TPU v7x, 128 devices: a whole 4x4x4 slice. The times are simulated.
128 devices in a mesh: row: 16 (over z, x), col: 8 (over y, core).
Axes of the slice: x: 4, y: 4, z: 4, core: 2. Of those that a mesh axis runs over, the one named last changes fastest.
Arguments:
- src_points: float32 [64, 16384], P(None, ('row', 'col')), as said below
- tgt_points: float32 [64, 32768], P(None, ('col', 'row')), as said below
- log_a: float32 [16384], P('row'), may hold values from -5 to 5
- log_b: float32 [32768], P('col'), may hold values from -5 to 5
- g_current: float32 [32768], P(('col', 'row')), may hold values from -4 to 4
- hist_g: float32 [4, 32768], P(None, ('col', 'row')), may hold values from -4 to 4
- hist_maps: float32 [4, 32768], P(None, ('col', 'row')), may hold values from -4 to 4
Outputs:
- f_out: float32 [16384], P('row')
- g_out: float32 [32768], P(('col', 'row'))
Inputs may be any that keep to these rules, and one draw needn't show every extreme that they name: `src_points`: coordinates of the source points. `tgt_points`: coordinates of the target points.
All inputs are finite; a program needn't handle non-finite values.
Results may differ from a plain program's by a relative error of at most 0.0003.
Values sent between devices are 32-bit elements; how exact they have to be, the bound alone decides.
A program may use at most 64 MiB of HBM per device.

v0:
```python
import functools

import jax
import jax.numpy as jnp
from jax import lax
from jax.sharding import Mesh
from jax.sharding import PartitionSpec as P

HIST = 5
ITERS = 2
COL = ("col_0", "col_1")
ROW = ("row_0", "row_1")
ROW_COL = ("row_0", "row_1", "col_0", "col_1")
COL_ROW = ("col_0", "col_1", "row_0", "row_1")


EPS = 0.1


def joined_along(blocks, dim):
    shape = list(blocks.shape[1:])
    shape[dim] *= blocks.shape[0]
    return jnp.moveaxis(blocks, 0, dim).reshape(shape)


def from_everyone(array, axis):
    copies = jnp.broadcast_to(array, (lax.axis_size(axis), *array.shape))
    return lax.all_to_all(copies, axis, split_axis=0, concat_axis=0, tiled=True)


def collect(array, axis, dim):
    return joined_along(from_everyone(array, axis), dim)


def combined_pairwise(pieces, combine):
    while len(jax.tree.leaves(pieces)[0]) > 1:
        pieces = jax.vmap(combine)(
            *(jax.tree.map(lambda part: part[side::2], pieces) for side in (0, 1))
        )
    return jax.tree.map(lambda part: part[0], pieces)


def merged(array, axis, combine):
    pieces = jax.tree.map(lambda part: from_everyone(part, axis), array)
    return combined_pairwise(pieces, combine)


def in_one_piece(arrays, axis, split_dim, concat_dim, along):
    both = jnp.concatenate(arrays, axis=along)
    filled, at, finished = (
        lax.all_to_all(both, axis, split_axis=split_dim, concat_axis=concat_dim, tiled=True),
        0,
        [],
    )
    for a in arrays:
        finished.append(lax.slice_in_dim(filled, at, at + a.shape[along], axis=along))
        at += a.shape[along]
    return tuple(finished)


def one_axis_at_a_time(array, axes):
    return functools.reduce(lax.psum, axes, array)


def cost_of(source, source_sq, target, target_sq):
    cross = lax.dot_general(
        source,
        target,
        (((0,), (0,)), ((), ())),
        precision=lax.Precision.HIGHEST,
        preferred_element_type=jnp.float32,
    )
    return source_sq[:, None] + target_sq[None, :] - 2.0 * cross


def combine(first, second):
    top = jnp.maximum(first[0], second[0])
    return (top, first[1] * jnp.exp(first[0] - top) + second[1] * jnp.exp(second[0] - top))


def solve_small(matrix, rhs):
    extent = matrix.shape[0]
    rows_list = [matrix[k] for k in range(extent)]
    values = [rhs[k] for k in range(extent)]
    for pivot_index in range(extent):
        for lower_row in range(pivot_index + 1, extent):
            factor = rows_list[lower_row][pivot_index] / rows_list[pivot_index][pivot_index]
            rows_list[lower_row] = rows_list[lower_row] - factor * rows_list[pivot_index]
            values[lower_row] = values[lower_row] - factor * values[pivot_index]
    answer = [None] * extent
    for pivot_index in reversed(range(extent)):
        running = values[pivot_index]
        for upper_col in range(pivot_index + 1, extent):
            running = running - rows_list[pivot_index][upper_col] * answer[upper_col]
        answer[pivot_index] = running / rows_list[pivot_index][pivot_index]
    return jnp.stack(answer)


def mix_weights(gram):
    extent = gram.shape[0]
    shift = 0.001 * jnp.trace(gram) / extent + 1e-06
    system = gram + shift * jnp.eye(extent, dtype=jnp.float32)
    weights = solve_small(system, jnp.ones((extent,), jnp.float32))
    return weights / jnp.sum(weights)


def shards(src_points, tgt_points, log_a, log_b, g_current, hist_g, hist_maps):
    source = lax.all_gather(src_points, COL, axis=1, tiled=True)
    target = collect(tgt_points, ROW, 1)
    source_sq = jnp.sum(source * source, axis=0)
    target_sq = jnp.sum(target * target, axis=0)
    row_count = source.shape[1]
    col_count = target.shape[1]
    block_rows = min(512, row_count)
    block_count = row_count // block_rows
    share_len = g_current.shape[0]
    row_devices = lax.axis_size(ROW)
    whole_tile = cost_of(source, source_sq, target, target_sq)

    def tile_piece(index):
        return lax.dynamic_slice_in_dim(whole_tile, index * block_rows, block_rows, 0)

    potentials = [hist_g[k] for k in range(hist_g.shape[0])]
    images = [hist_maps[k] for k in range(hist_maps.shape[0])]
    g_share = g_current
    f_whole = None
    for turn_index in range(ITERS):
        g_block = collect(g_share, ROW, 0)
        column_term = g_block / EPS + log_b

        def row_part(index):
            scores = column_term[None, :] - tile_piece(index) / EPS
            top = jnp.max(scores, axis=1)
            return (top, jnp.sum(jnp.exp(scores - top[:, None]), axis=1))

        row_top, row_total = lax.map(row_part, jnp.arange(block_count, dtype=jnp.int32))
        row_top, row_total = merged((row_top.reshape(-1), row_total.reshape(-1)), COL, combine)
        f_whole = -EPS * (row_top + jnp.log(row_total))
        row_term = f_whole / EPS + log_a

        def column_step(carry, index):
            term_piece = lax.dynamic_slice_in_dim(row_term, index * block_rows, block_rows, 0)
            scores = term_piece[:, None] - tile_piece(index) / EPS
            top = jnp.max(scores, axis=0)
            partial_value = (top, jnp.sum(jnp.exp(scores - top[None, :]), axis=0))
            return (combine(carry, partial_value), None)

        start_carry = (
            jnp.full((col_count,), -jnp.inf, jnp.float32),
            jnp.zeros((col_count,), jnp.float32),
        )
        (col_top, col_total), unused = lax.scan(
            column_step, start_carry, jnp.arange(block_count, dtype=jnp.int32)
        )
        part_top, part_total = in_one_piece(
            (col_top.reshape(row_devices, share_len), col_total.reshape(row_devices, share_len)),
            ROW,
            0,
            0,
            1,
        )
        best = jnp.max(part_top, axis=0)
        mapped = -EPS * (
            best + jnp.log(jnp.sum(part_total * jnp.exp(part_top - best[None, :]), axis=0))
        )
        potentials = (potentials + [g_share])[-HIST:]
        images = (images + [mapped])[-HIST:]
        image_stack = jnp.stack(images)
        resid = image_stack - jnp.stack(potentials)
        local_gram = jnp.dot(
            resid, resid.T, precision=lax.Precision.HIGHEST, preferred_element_type=jnp.float32
        )
        gram = one_axis_at_a_time(local_gram, ROW_COL)
        mix = mix_weights(gram)
        g_share = jnp.dot(
            mix, image_stack, precision=lax.Precision.HIGHEST, preferred_element_type=jnp.float32
        )
    return (f_whole, g_share)


def solution(mesh):
    split = Mesh(mesh.devices.reshape(4, 4, 4, 2), ("row_0", "row_1", "col_0", "col_1"))
    in_specs = (
        P(None, ROW_COL),
        P(None, COL_ROW),
        P(ROW),
        P(COL),
        P(COL_ROW),
        P(None, COL_ROW),
        P(None, COL_ROW),
    )
    out_specs = (P(ROW), P(COL_ROW))
    return jax.shard_map(
        shards, mesh=split, in_specs=in_specs, out_specs=out_specs, check_vma=False
    )
```

profile of v0, /device:TPU:1, one launch (start us, length us, event | category | flops | bytes accessed | tf_op | source)
XLA Modules:
  0.0 333.7 jit_solution(7343399051861409410)
XLA Ops:
  1.3 14.7 %all_to_all.77 = f32[16,1,256]{2,1,0:T(1,128)S(1)} all-to-all(f32[16,1,256]{2,1,0:T(1,128)S(1)} %broadcast_in_dim.54), channel_id=1, replica_groups=mesh['row_0'=4,'row_1'=4,'col_0'=4,'col_1'=2] {'row_0','row_1'}, dimensions={0} | all-to-all | bytes 32768 | tf_op jit(solution)/shard_map/all_to_all | solution.py:28
  16.0 1.9 broadcast_in_dim.55
  17.9 3.7 %all-to-all-start.1 = ((f32[16,64,256]{2,1,0:T(8,128)}), f32[16,64,256]{2,1,0:T(8,128)S(1)}, u32[]{:S(2)}, u32[]{:S(2)}) async-start(f32[16,64,256]{2,1,0:T(8,128)} %broadcast_in_dim.55), calls=%async_computation.1 | async-start | bytes 2097152 | tf_op jit(solution)/shard_map/all_to_all | solution.py:28
  21.6 15.5 %all_gather.3 = f32[64,1024]{1,0:T(8,128)S(1)} all-gather(f32[64,128]{1,0:T(8,128)} %param.15), channel_id=1, replica_groups=mesh['row_0'=4,'row_1'=4,'col_0'=4,'col_1'=2] {'col_0','col_1'}, dimensions={1}, use_global_device_ids=true | all-gather | bytes 294912 | tf_op jit(solution)/shard_map/all_gather | solution.py:108
  37.1 0.7 add.135
  38.1 16.6 %multiply_subtract_fusion.4 = f32[1024,4096]{1,0:T(8,128)} fusion(f32[64,1024]{1,0:T(8,128)S(1)} %all_gather.3, f32[64,4096]{1,0:T(8,128)S(1)} %bitcast.137, f32[4096]{0:T(1024)S(1)} %bitcast.140, f32[1024]{0:T(1024)S(1)} %multiply_reduce_fusion), kind=kOutput, calls=%fused_computation.18 | convolution fusion | flops 3233808384 | bytes 18108416 | tf_op jit(solution)/shard_map/dot_general | solution.py:66
  54.7 20.1 %while.50 = (s32[]{:T(128)}, f32[2,512]{1,0:T(2,128)S(1)}, f32[2,512]{1,0:T(2,128)S(1)}, f32[4096]{0:T(1024)S(1)}, s32[2]{0:T(128)S(1)}, /*index=5*/f32[1024,409...) while((s32[]{:T(128)}, f32[2,512]{1,0:T(2,128)S(1)}, f32[2,512]{1,0:T(2,128)S(1)}, ...), condition=%wide.region_5.6_spmd, body=%wide.region_2.5_spmd.sunk | while | flops 14679046 | bytes 16824496 | solution.py:136
  55.9 4.3 %fusion.52 = f32[512]{0:T(512)S(1)} fusion(f32[1024,4096]{1,0:T(8,128)} %get-tuple-element.481, s32[]{:T(128)S(6)} %select_n.32, f32[4096]{0:T(1024)S(1)} %get-tuple-element.479), kind=kLoop, calls=%fused_computation.2.clone.1 | loop fusion | flops 6290944 | bytes 8407044 | tf_op jit(solution)/shard_map/while/body/eval_jaxpr/reduce_max | solution.py:133
  60.2 4.4 %exponential_reduce_fusion.8 = f32[512]{0:T(512)S(1)} fusion(f32[1024,4096]{1,0:T(8,128)} %get-tuple-element.481, s32[]{:T(128)S(6)} %select_n.32, f32[512]{0:T(512)S(1)} %fusion.52, f32[4096]{0:T(1024)S(1)} %get-tuple-element.479), kind=kLoop, calls=%fused_computation.clone.1 | loop fusion | flops 8388096 | bytes 8409092 | tf_op jit(solution)/shard_map/while/body/eval_jaxpr/reduce_sum | solution.py:134
  66.0 4.3 %fusion.52 = f32[512]{0:T(512)S(1)} fusion(f32[1024,4096]{1,0:T(8,128)} %get-tuple-element.481, s32[]{:T(128)S(6)} %select_n.32, f32[4096]{0:T(1024)S(1)} %get-tuple-element.479), kind=kLoop, calls=%fused_computation.2.clone.1 | loop fusion | flops 6290944 | bytes 8407044 | tf_op jit(solution)/shard_map/while/body/eval_jaxpr/reduce_max | solution.py:133
  70.3 4.4 %exponential_reduce_fusion.8 = f32[512]{0:T(512)S(1)} fusion(f32[1024,4096]{1,0:T(8,128)} %get-tuple-element.481, s32[]{:T(128)S(6)} %select_n.32, f32[512]{0:T(512)S(1)} %fusion.52, f32[4096]{0:T(1024)S(1)} %get-tuple-element.479), kind=kLoop, calls=%fused_computation.clone.1 | loop fusion | flops 8388096 | bytes 8409092 | tf_op jit(solution)/shard_map/while/body/eval_jaxpr/reduce_sum | solution.py:134
  75.4 6.5 %all-to-all-start.2 = ((f32[8,1,1024]{2,1,0:T(1,128)}), f32[8,1,1024]{2,1,0:T(1,128)S(1)}, u32[]{:S(2)}, u32[]{:S(2)}) async-start(f32[8,1,1024]{2,1,0:T(1,128)} %broadcast_in_dim.57), calls=%async_computation.2 | async-start | bytes 65536 | tf_op jit(solution)/shard_map/all_to_all | solution.py:28
  82.0 4.7 %all-to-all-done.2 = f32[8,1,1024]{2,1,0:T(1,128)S(1)} async-done(((f32[8,1,1024]{2,1,0:T(1,128)}), f32[8,1,1024]{2,1,0:T(1,128)S(1)}, u32[]{:S(2)}, u32[]{:S(2)}) %all-to-all-start.2) | async-done | bytes 32800 | tf_op jit(solution)/shard_map/all_to_all | solution.py:28
  87.3 4.0 %all-to-all-start.3 = ((f32[8,1,1024]{2,1,0:T(1,128)}), f32[8,1,1024]{2,1,0:T(1,128)S(1)}, u32[]{:S(2)}, u32[]{:S(2)}) async-start(f32[8,1,1024]{2,1,0:T(1,128)} %broadcast_in_dim.59), calls=%async_computation.3 | async-start | bytes 65536 | tf_op jit(solution)/shard_map/all_to_all | solution.py:28
  91.3 4.7 %all-to-all-done.3 = f32[8,1,1024]{2,1,0:T(1,128)S(1)} async-done(((f32[8,1,1024]{2,1,0:T(1,128)}), f32[8,1,1024]{2,1,0:T(1,128)S(1)}, u32[]{:S(2)}, u32[]{:S(2)}) %all-to-all-start.3) | async-done | bytes 32800 | tf_op jit(solution)/shard_map/all_to_all | solution.py:28
  96.4 20.7 %while.52 = (s32[]{:T(128)}, f32[4096]{0:T(1024)S(1)}, f32[4096]{0:T(1024)S(1)}, s32[2]{0:T(128)S(1)}, f32[1024]{0:T(1024)S(1)}, /*index=5*/f32[1024,4096]{1,0:T...) while((s32[]{:T(128)}, f32[4096]{0:T(1024)S(1)}, f32[4096]{0:T(1024)S(1)}, s32[2]{0:T(128)S(1)}, ...), condition=%wide.region_9.10_spmd.clone, body=%wide.region_6.9_spmd.clone.sunk | while | flops 14704647 | bytes 16933044 | solution.py:152
  97.7 4.6 %fusion.54 = f32[4096]{0:T(1024)S(1)} fusion(f32[1024,4096]{1,0:T(8,128)} %get-tuple-element.511, s32[]{:T(128)S(6)} %select_n.34, f32[512]{0:T(512)S(1)} %dynamic_slice.80), kind=kLoop, calls=%fused_computation.8.clone.1 | loop fusion | flops 6287360 | bytes 8407044 | tf_op jit(solution)/shard_map/while/body/eval_jaxpr/reduce_max | solution.py:144
  102.3 4.4 %exponential_reduce_fusion.10 = f32[4096]{0:T(1024)S(1)} fusion(f32[1024,4096]{1,0:T(8,128)} %get-tuple-element.511, s32[]{:T(128)S(6)} %select_n.34, f32[4096]{0:T(1024)S(1)} %fusion.54, f32[512]{0:T(512)S(1)} %dynamic_slice.80), kind=kLoop, calls=%fused_computation.6.clone.1 | loop fusion | flops 8384512 | bytes 8423428 | tf_op jit(solution)/shard_map/while/body/eval_jaxpr/reduce_sum | solution.py:145
  108.0 4.6 %fusion.54 = f32[4096]{0:T(1024)S(1)} fusion(f32[1024,4096]{1,0:T(8,128)} %get-tuple-element.511, s32[]{:T(128)S(6)} %select_n.34, f32[512]{0:T(512)S(1)} %dynamic_slice.80), kind=kLoop, calls=%fused_computation.8.clone.1 | loop fusion | flops 6287360 | bytes 8407044 | tf_op jit(solution)/shard_map/while/body/eval_jaxpr/reduce_max | solution.py:144
  112.6 4.4 %exponential_reduce_fusion.10 = f32[4096]{0:T(1024)S(1)} fusion(f32[1024,4096]{1,0:T(8,128)} %get-tuple-element.511, s32[]{:T(128)S(6)} %select_n.34, f32[4096]{0:T(1024)S(1)} %fusion.54, f32[512]{0:T(512)S(1)} %dynamic_slice.80), kind=kLoop, calls=%fused_computation.6.clone.1 | loop fusion | flops 8384512 | bytes 8423428 | tf_op jit(solution)/shard_map/while/body/eval_jaxpr/reduce_sum | solution.py:145
  117.1 10.5 %all_to_all.78 = f32[16,1,512]{2,1,0:T(1,128)S(1)} all-to-all(f32[16,1,512]{2,1,0:T(1,128)S(1)} %all_to_all.57), channel_id=1, replica_groups=mesh['row_0'=4,'row_1'=4,'col_0'=4,'col_1'=2] {'row_0','row_1'}, dimensions={0} | all-to-all | bytes 65536 | tf_op jit(solution)/shard_map/all_to_all | solution.py:51
  127.9 6.9 %psum.56 = f32[5,5]{1,0:T(8,128)S(1)} all-reduce(f32[5,5]{1,0:T(8,128)S(1)} %fusion.11), channel_id=1, replica_groups=mesh['row_0'=4,'row_1'=4,'col_0'=4,'col_1'=2] {'row_0'}, use_global_device_ids=true, to_apply=%region_12.13 | all-reduce | flops 25 | bytes 200 | tf_op jit(solution)/shard_map/psum | solution.py:62
  134.7 6.9 %psum.57 = f32[5,5]{1,0:T(8,128)S(1)} all-reduce(f32[5,5]{1,0:T(8,128)S(1)} %psum.56), channel_id=1, replica_groups=mesh['row_0'=4,'row_1'=4,'col_0'=4,'col_1'=2] {'row_1'}, use_global_device_ids=true, to_apply=%region_13.14 | all-reduce | flops 25 | bytes 200 | tf_op jit(solution)/shard_map/psum | solution.py:62
  141.6 6.9 %psum.58 = f32[5,5]{1,0:T(8,128)S(1)} all-reduce(f32[5,5]{1,0:T(8,128)S(1)} %psum.57), channel_id=1, replica_groups=mesh['row_0'=4,'row_1'=4,'col_0'=4,'col_1'=2] {'col_0'}, use_global_device_ids=true, to_apply=%region_14.15 | all-reduce | flops 25 | bytes 200 | tf_op jit(solution)/shard_map/psum | solution.py:62
  148.5 10.3 %psum.59 = f32[5,5]{1,0:T(8,128)S(1)} all-reduce(f32[5,5]{1,0:T(8,128)S(1)} %psum.58), channel_id=1, replica_groups=mesh['row_0'=4,'row_1'=4,'col_0'=4,'col_1'=2] {'col_1'}, use_global_device_ids=true, to_apply=%region_15.16 | all-reduce | flops 25 | bytes 200 | tf_op jit(solution)/shard_map/psum | solution.py:62
  190.3 3.7 %all-to-all-start.5 = ((f32[16,1,256]{2,1,0:T(1,128)}), f32[16,1,256]{2,1,0:T(1,128)S(1)}, u32[]{:S(2)}, u32[]{:S(2)}) async-start(f32[16,1,256]{2,1,0:T(1,128)} %broadcast_in_dim.60), calls=%async_computation.5 | async-start | bytes 32768 | tf_op jit(solution)/shard_map/all_to_all | solution.py:28
  194.0 6.2 %all-to-all-done.5 = f32[16,1,256]{2,1,0:T(1,128)S(1)} async-done(((f32[16,1,256]{2,1,0:T(1,128)}), f32[16,1,256]{2,1,0:T(1,128)S(1)}, u32[]{:S(2)}, u32[]{:S(2)}) %all-to-all-start.5) | async-done | bytes 16416 | tf_op jit(solution)/shard_map/all_to_all | solution.py:28
  200.2 20.1 %while.51 = (s32[]{:T(128)}, f32[2,512]{1,0:T(2,128)S(1)}, f32[2,512]{1,0:T(2,128)S(1)}, f32[4096]{0:T(1024)S(1)}, s32[2]{0:T(128)S(1)}, /*index=5*/f32[1024,409...) while((s32[]{:T(128)}, f32[2,512]{1,0:T(2,128)S(1)}, f32[2,512]{1,0:T(2,128)S(1)}, ...), condition=%wide.region_20.21_spmd, body=%wide.region_17.20_spmd.sunk | while | flops 14679046 | bytes 16824496 | solution.py:136
  201.5 4.3 %fusion.53 = f32[512]{0:T(512)S(1)} fusion(f32[1024,4096]{1,0:T(8,128)} %get-tuple-element.541, s32[]{:T(128)S(6)} %select_n.33, f32[4096]{0:T(1024)S(1)} %get-tuple-element.539), kind=kLoop, calls=%fused_computation.5.clone.1 | loop fusion | flops 6290944 | bytes 8407044 | tf_op jit(solution)/shard_map/while/body/eval_jaxpr/reduce_max | solution.py:133
  205.8 4.4 %exponential_reduce_fusion.9 = f32[512]{0:T(512)S(1)} fusion(f32[1024,4096]{1,0:T(8,128)} %get-tuple-element.541, s32[]{:T(128)S(6)} %select_n.33, f32[512]{0:T(512)S(1)} %fusion.53, f32[4096]{0:T(1024)S(1)} %get-tuple-element.539), kind=kLoop, calls=%fused_computation.3.clone.1 | loop fusion | flops 8388096 | bytes 8409092 | tf_op jit(solution)/shard_map/while/body/eval_jaxpr/reduce_sum | solution.py:134
  211.6 4.3 %fusion.53 = f32[512]{0:T(512)S(1)} fusion(f32[1024,4096]{1,0:T(8,128)} %get-tuple-element.541, s32[]{:T(128)S(6)} %select_n.33, f32[4096]{0:T(1024)S(1)} %get-tuple-element.539), kind=kLoop, calls=%fused_computation.5.clone.1 | loop fusion | flops 6290944 | bytes 8407044 | tf_op jit(solution)/shard_map/while/body/eval_jaxpr/reduce_max | solution.py:133
  215.8 4.4 %exponential_reduce_fusion.9 = f32[512]{0:T(512)S(1)} fusion(f32[1024,4096]{1,0:T(8,128)} %get-tuple-element.541, s32[]{:T(128)S(6)} %select_n.33, f32[512]{0:T(512)S(1)} %fusion.53, f32[4096]{0:T(1024)S(1)} %get-tuple-element.539), kind=kLoop, calls=%fused_computation.3.clone.1 | loop fusion | flops 8388096 | bytes 8409092 | tf_op jit(solution)/shard_map/while/body/eval_jaxpr/reduce_sum | solution.py:134
  221.0 4.7 %all-to-all-start.6 = ((f32[8,1,1024]{2,1,0:T(1,128)}), f32[8,1,1024]{2,1,0:T(1,128)S(1)}, u32[]{:S(2)}, u32[]{:S(2)}) async-start(f32[8,1,1024]{2,1,0:T(1,128)} %broadcast_in_dim.62), calls=%async_computation.6 | async-start | bytes 65536 | tf_op jit(solution)/shard_map/all_to_all | solution.py:28
  225.7 4.7 %all-to-all-done.6 = f32[8,1,1024]{2,1,0:T(1,128)S(1)} async-done(((f32[8,1,1024]{2,1,0:T(1,128)}), f32[8,1,1024]{2,1,0:T(1,128)S(1)}, u32[]{:S(2)}, u32[]{:S(2)}) %all-to-all-start.6) | async-done | bytes 32800 | tf_op jit(solution)/shard_map/all_to_all | solution.py:28
  231.1 4.0 %all-to-all-start.7 = ((f32[8,1,1024]{2,1,0:T(1,128)}), f32[8,1,1024]{2,1,0:T(1,128)S(1)}, u32[]{:S(2)}, u32[]{:S(2)}) async-start(f32[8,1,1024]{2,1,0:T(1,128)} %broadcast_in_dim.64), calls=%async_computation.7 | async-start | bytes 65536 | tf_op jit(solution)/shard_map/all_to_all | solution.py:28
  235.1 4.7 %all-to-all-done.7 = f32[8,1,1024]{2,1,0:T(1,128)S(1)} async-done(((f32[8,1,1024]{2,1,0:T(1,128)}), f32[8,1,1024]{2,1,0:T(1,128)S(1)}, u32[]{:S(2)}, u32[]{:S(2)}) %all-to-all-start.7) | async-done | bytes 32800 | tf_op jit(solution)/shard_map/all_to_all | solution.py:28
  240.1 20.7 %while.53 = (s32[]{:T(128)}, f32[4096]{0:T(1024)S(1)}, f32[4096]{0:T(1024)S(1)}, s32[2]{0:T(128)S(1)}, f32[1024]{0:T(1024)S(1)}, /*index=5*/f32[1024,4096]{1,0:T...) while((s32[]{:T(128)}, f32[4096]{0:T(1024)S(1)}, f32[4096]{0:T(1024)S(1)}, s32[2]{0:T(128)S(1)}, ...), condition=%wide.region_24.25_spmd.clone, body=%wide.region_21.24_spmd.clone.sunk | while | flops 14704647 | bytes 16933044 | solution.py:152
  241.4 4.6 %fusion.56 = f32[4096]{0:T(1024)S(1)} fusion(f32[1024,4096]{1,0:T(8,128)} %get-tuple-element.571, s32[]{:T(128)S(6)} %select_n.35, f32[512]{0:T(512)S(1)} %dynamic_slice.84), kind=kLoop, calls=%fused_computation.14.clone.1 | loop fusion | flops 6287360 | bytes 8407044 | tf_op jit(solution)/shard_map/while/body/eval_jaxpr/reduce_max | solution.py:144
  246.0 4.4 %exponential_reduce_fusion.11 = f32[4096]{0:T(1024)S(1)} fusion(f32[1024,4096]{1,0:T(8,128)} %get-tuple-element.571, s32[]{:T(128)S(6)} %select_n.35, f32[4096]{0:T(1024)S(1)} %fusion.56, f32[512]{0:T(512)S(1)} %dynamic_slice.84), kind=kLoop, calls=%fused_computation.12.clone.1 | loop fusion | flops 8384512 | bytes 8423428 | tf_op jit(solution)/shard_map/while/body/eval_jaxpr/reduce_sum | solution.py:145
  251.8 4.6 %fusion.56 = f32[4096]{0:T(1024)S(1)} fusion(f32[1024,4096]{1,0:T(8,128)} %get-tuple-element.571, s32[]{:T(128)S(6)} %select_n.35, f32[512]{0:T(512)S(1)} %dynamic_slice.84), kind=kLoop, calls=%fused_computation.14.clone.1 | loop fusion | flops 6287360 | bytes 8407044 | tf_op jit(solution)/shard_map/while/body/eval_jaxpr/reduce_max | solution.py:144
  256.3 4.4 %exponential_reduce_fusion.11 = f32[4096]{0:T(1024)S(1)} fusion(f32[1024,4096]{1,0:T(8,128)} %get-tuple-element.571, s32[]{:T(128)S(6)} %select_n.35, f32[4096]{0:T(1024)S(1)} %fusion.56, f32[512]{0:T(512)S(1)} %dynamic_slice.84), kind=kLoop, calls=%fused_computation.12.clone.1 | loop fusion | flops 8384512 | bytes 8423428 | tf_op jit(solution)/shard_map/while/body/eval_jaxpr/reduce_sum | solution.py:145
  261.4 3.5 %all-to-all-start.8 = ((f32[16,1,512]{2,1,0:T(1,128)}), f32[16,1,512]{2,1,0:T(1,128)S(1)}, u32[]{:S(2)}, u32[]{:S(2)}) async-start(f32[16,1,512]{2,1,0:T(1,128)} %all_to_all.65), calls=%async_computation.8 | async-start | bytes 65536 | tf_op jit(solution)/shard_map/all_to_all | solution.py:51
  265.5 5.8 %all-to-all-done.8 = f32[16,1,512]{2,1,0:T(1,128)S(1)} async-done(((f32[16,1,512]{2,1,0:T(1,128)}), f32[16,1,512]{2,1,0:T(1,128)S(1)}, u32[]{:S(2)}, u32[]{:S(2)}) %all-to-all-start.8) | async-done | bytes 32800 | tf_op jit(solution)/shard_map/all_to_all | solution.py:51
  271.5 6.8 %psum.60 = f32[5,5]{1,0:T(8,128)S(1)} all-reduce(f32[5,5]{1,0:T(8,128)S(1)} %fusion.16), channel_id=1, replica_groups=mesh['row_0'=4,'row_1'=4,'col_0'=4,'col_1'=2] {'row_0'}, use_global_device_ids=true, to_apply=%region_27.28 | all-reduce | flops 25 | bytes 200 | tf_op jit(solution)/shard_map/psum | solution.py:62
  278.4 6.9 %psum.61 = f32[5,5]{1,0:T(8,128)S(1)} all-reduce(f32[5,5]{1,0:T(8,128)S(1)} %psum.60), channel_id=1, replica_groups=mesh['row_0'=4,'row_1'=4,'col_0'=4,'col_1'=2] {'row_1'}, use_global_device_ids=true, to_apply=%region_28.29 | all-reduce | flops 25 | bytes 200 | tf_op jit(solution)/shard_map/psum | solution.py:62
  285.3 6.9 %psum.62 = f32[5,5]{1,0:T(8,128)S(1)} all-reduce(f32[5,5]{1,0:T(8,128)S(1)} %psum.61), channel_id=1, replica_groups=mesh['row_0'=4,'row_1'=4,'col_0'=4,'col_1'=2] {'col_0'}, use_global_device_ids=true, to_apply=%region_29.30 | all-reduce | flops 25 | bytes 200 | tf_op jit(solution)/shard_map/psum | solution.py:62
  292.1 10.1 %psum.63 = f32[5,5]{1,0:T(8,128)S(1)} all-reduce(f32[5,5]{1,0:T(8,128)S(1)} %psum.62), channel_id=1, replica_groups=mesh['row_0'=4,'row_1'=4,'col_0'=4,'col_1'=2] {'col_1'}, use_global_device_ids=true, to_apply=%region_30.31 | all-reduce | flops 25 | bytes 200 | tf_op jit(solution)/shard_map/psum | solution.py:62
  333.0 0.7 fusion.21
  (150 shorter events, 27.2 us)
Async XLA Ops:
  17.9 20.0 %all-to-all-start.1 = ((f32[16,64,256]{2,1,0:T(8,128)}), f32[16,64,256]{2,1,0:T(8,128)S(1)}, u32[]{:S(2)}, u32[]{:S(2)}) async-start(f32[16,64,256]{2,1,0:T(8,128)} %broadcast_in_dim.55), calls=%async_computation.1 | async-start | bytes 2097152 | tf_op jit(solution)/shard_map/all_to_all | solution.py:28
  54.7 41.6 %copy-start.1 = (f32[1024]{0:T(1024)S(1)}, f32[1024]{0:T(1024)}, u32[]{:S(2)}) copy-start(f32[1024]{0:T(1024)} %param.17) | copy-start | bytes 12292
  75.4 11.3 %all-to-all-start.2 = ((f32[8,1,1024]{2,1,0:T(1,128)}), f32[8,1,1024]{2,1,0:T(1,128)S(1)}, u32[]{:S(2)}, u32[]{:S(2)}) async-start(f32[8,1,1024]{2,1,0:T(1,128)} %broadcast_in_dim.57), calls=%async_computation.2 | async-start | bytes 65536 | tf_op jit(solution)/shard_map/all_to_all | solution.py:28
  87.3 8.7 %all-to-all-start.3 = ((f32[8,1,1024]{2,1,0:T(1,128)}), f32[8,1,1024]{2,1,0:T(1,128)S(1)}, u32[]{:S(2)}, u32[]{:S(2)}) async-start(f32[8,1,1024]{2,1,0:T(1,128)} %broadcast_in_dim.59), calls=%async_computation.3 | async-start | bytes 65536 | tf_op jit(solution)/shard_map/all_to_all | solution.py:28
  96.3 31.4 %copy-start.2 = (f32[4,256]{1,0:T(4,128)S(1)}, f32[4,256]{1,0:T(4,128)}, u32[]{:S(2)}) copy-start(f32[4,256]{1,0:T(4,128)} %param.21) | copy-start | bytes 12292
  96.3 31.4 %copy-start.3 = (f32[4,256]{1,0:T(4,128)S(1)}, f32[4,256]{1,0:T(4,128)}, u32[]{:S(2)}) copy-start(f32[4,256]{1,0:T(4,128)} %param.20) | copy-start | bytes 12292
  96.3 31.4 %copy-start.4 = (f32[256]{0:T(256)S(1)}, f32[256]{0:T(256)}, u32[]{:S(2)}) copy-start(f32[256]{0:T(256)} %param.19) | copy-start | bytes 3076
  96.3 103.8 %copy-start = (f32[4096]{0:T(1024)S(1)}, f32[4096]{0:T(1024)}, u32[]{:S(2)}) copy-start(f32[4096]{0:T(1024)} %param.18) | copy-start | bytes 49156
  190.3 9.9 %all-to-all-start.5 = ((f32[16,1,256]{2,1,0:T(1,128)}), f32[16,1,256]{2,1,0:T(1,128)S(1)}, u32[]{:S(2)}, u32[]{:S(2)}) async-start(f32[16,1,256]{2,1,0:T(1,128)} %broadcast_in_dim.60), calls=%async_computation.5 | async-start | bytes 32768 | tf_op jit(solution)/shard_map/all_to_all | solution.py:28
  221.0 9.5 %all-to-all-start.6 = ((f32[8,1,1024]{2,1,0:T(1,128)}), f32[8,1,1024]{2,1,0:T(1,128)S(1)}, u32[]{:S(2)}, u32[]{:S(2)}) async-start(f32[8,1,1024]{2,1,0:T(1,128)} %broadcast_in_dim.62), calls=%async_computation.6 | async-start | bytes 65536 | tf_op jit(solution)/shard_map/all_to_all | solution.py:28
  231.1 8.7 %all-to-all-start.7 = ((f32[8,1,1024]{2,1,0:T(1,128)}), f32[8,1,1024]{2,1,0:T(1,128)S(1)}, u32[]{:S(2)}, u32[]{:S(2)}) async-start(f32[8,1,1024]{2,1,0:T(1,128)} %broadcast_in_dim.64), calls=%async_computation.7 | async-start | bytes 65536 | tf_op jit(solution)/shard_map/all_to_all | solution.py:28
  261.4 9.9 %all-to-all-start.8 = ((f32[16,1,512]{2,1,0:T(1,128)}), f32[16,1,512]{2,1,0:T(1,128)S(1)}, u32[]{:S(2)}, u32[]{:S(2)}) async-start(f32[16,1,512]{2,1,0:T(1,128)} %all_to_all.65), calls=%async_computation.8 | async-start | bytes 65536 | tf_op jit(solution)/shard_map/all_to_all | solution.py:51
where the time goes:
time: 336 us; the launch traced here: 334 us
  blocking collectives  102 us (30%)
  other arithmetic  73.9 us (22%)
  between operations  47.3 us (14%)
  waiting for transfers between devices  30.8 us (9%)
  starting transfers between devices  30 us (9%)
  local copies, waits for them, and re-layouts  26.3 us (8%)
  matrix products  17.7 us (5%)
  loops' own time  5.46 us (2%)
    psum x8, blocking collectives, one_axis_at_a_time(): return functools.reduce(lax.psum, axes, array)  61.6 us
    all_to_all x6, starting transfers between devices, from_everyone(): return lax.all_to_all(copies, axis, split_axis=0, concat_axis=0, tiled=True)  26.5 us
    all_to_all x6, waiting for transfers between devices, from_everyone(): return lax.all_to_all(copies, axis, split_axis=0, concat_axis=0, tiled=True)  25 us
    reduce_max x4, other arithmetic, column_step(): top = jnp.max(scores, axis=0)  18.2 us
    reduce_sum x4, other arithmetic, row_part(): return (top, jnp.sum(jnp.exp(scores - top[:, None]), axis=1))  17.8 us
    reduce_sum x4, other arithmetic, column_step(): partial_value = (top, jnp.sum(jnp.exp(scores - top[None, :]), axis=0))  17.6 us
    reduce_max x4, other arithmetic, row_part(): top = jnp.max(scores, axis=1)  17.1 us
    dot_general x1, matrix products, cost_of(): lax.dot_general(source, target, (((0,), (0,)), ((), ())), precision=lax.P...  16.6 us
  transfers between devices with their start and end apart: 7, of which 6 were waited for; matrix products, arithmetic and copies ran while one was open for 0% of the time, Pallas kernels for 0%

commit v1 on v0

v1 whole, which is shorter than its diff:
```python
import functools

import jax
import jax.numpy as jnp
from jax import lax
from jax.experimental import pallas as pl
from jax.experimental.pallas import tpu as pltpu
from jax.sharding import Mesh
from jax.sharding import PartitionSpec as P

HIST = 5
ITERS = 2
EPS = 0.1
LOG2E = 1.4426950408889634
BITS = LOG2E / EPS
NATS = EPS / LOG2E
MESH = pl.DeviceIdType.MESH
AXES = ("z", "x", "y", "core")


def split2(v):
    hi = v.astype(jnp.bfloat16).astype(jnp.float32)
    return hi, v - hi


def split3(v):
    hi = v.astype(jnp.bfloat16).astype(jnp.float32)
    rest = v - hi
    mid = rest.astype(jnp.bfloat16).astype(jnp.float32)
    return hi, mid, rest - mid


def placed(rows, values, width):
    at = lax.broadcasted_iota(jnp.int32, (rows, width), 0)
    out = jnp.zeros((rows, width), jnp.float32)
    for k, v in enumerate(values):
        out = jnp.where(at == k, v, out)
    return out


def gray(k):
    return k + (k // 2) * (5 - 2 * k)


def solve(gram):
    n = HIST
    trace = gram[0, 0]
    for k in range(1, n):
        trace = trace + gram[k, k]
    shift = 0.001 * trace / n + 1e-6
    a = [[gram[min(p, q), max(p, q)] + (shift if p == q else 0.0) for q in range(n)] for p in range(n)]
    rhs = [jnp.ones((1, 1), jnp.float32) for _ in range(n)]
    for p in range(n):
        for low in range(p + 1, n):
            factor = a[low][p] / a[p][p]
            for q in range(p + 1, n):
                a[low][q] = a[low][q] - factor * a[p][q]
            rhs[low] = rhs[low] - factor * rhs[p]
    out = [None] * n
    for p in reversed(range(n)):
        acc = rhs[p]
        for q in range(p + 1, n):
            acc = acc - a[p][q] * out[q]
        out[p] = acc / a[p][p]
    total = out[0]
    for k in range(1, n):
        total = total + out[k]
    return [o / total for o in out]


def kernel(
    dims,
    src_ref, tgt_ref, loga_ref, logb_ref, g_ref, hg_ref, hm_ref,
    f_ref, gout_ref,
    tgt_all, src_all, lhs, zs, mrep, sacc, bias, delta,
    f_buf, c_send, c_buf, m_buf, r_buf,
    tgt_send, tgt_recv, src_send, src_recv, f_sems, c_sems, m_sems, r_sems,
):
    NZ, NX, NY, NC = dims
    NR, NK = NZ * NX, NY * NC
    D, SW = src_ref.shape
    TW = tgt_ref.shape[1]
    ROWS = NK * SW
    z, x = lax.axis_index("z"), lax.axis_index("x")
    y, core = lax.axis_index("y"), lax.axis_index("core")
    row, col = z * NX + x, y * NC + core

    def row_peer(k):
        p = lax.rem(row + k, NR)
        return {"z": p // NX, "x": lax.rem(p, NX)}

    def col_peer(k):
        p = lax.rem(col + k, NK)
        return {"y": p // NC, "core": lax.rem(p, NC)}

    def to_all(peer, count, src, dst, ssem, rsem):
        def one(k, carry):
            pltpu.make_async_remote_copy(
                src_ref=src(k), dst_ref=dst, send_sem=ssem, recv_sem=rsem,
                device_id=peer(k), device_id_type=MESH,
            ).start()
            return carry
        lax.fori_loop(1, count, one, 0)

    def wait_bytes(buf, count, sem):
        part = buf.at[pl.ds(0, count)]
        pltpu.make_async_copy(part, part, sem).wait()

    mine = tgt_all.at[row]
    mine[0:D, :] = tgt_ref[...]
    mine[D:D + 8, :] = placed(8, [g_ref[...]] + [hm_ref[k:k + 1, :] for k in range(HIST - 1)], TW)
    src_all[col] = src_ref[...]

    barrier = pltpu.get_barrier_semaphore()

    def greet(peer):
        def one(k, carry):
            pl.semaphore_signal(barrier, inc=1, device_id=peer(k), device_id_type=MESH)
            return carry
        return one
    lax.fori_loop(1, NR, greet(row_peer), 0)
    lax.fori_loop(1, NK, greet(col_peer), 0)
    pl.semaphore_wait(barrier, NR + NK - 2)

    to_all(col_peer, NK, lambda k: src_all.at[col], src_all.at[col], src_send, src_recv)
    to_all(row_peer, NR, lambda k: tgt_all.at[row], tgt_all.at[row], tgt_send, tgt_recv.at[row])

    wait_bytes(src_all, NK - 1, src_recv)

    def left(b, carry):
        v = src_all[b]
        norm = jnp.sum(v * v, axis=0, keepdims=True) * (-BITS)
        hi, lo = split2(v * (2.0 * BITS))
        one = jnp.ones((1, SW), jnp.float32)
        tail = placed(D, list(split3(norm)) + [one] * 6, SW)
        full = jnp.concatenate([hi, hi, lo, tail], axis=0)
        lhs[pl.ds(pl.multiple_of(b * SW, SW), SW), :] = full.T.astype(jnp.bfloat16)
        return carry
    lax.fori_loop(0, NK, left, 0)

    mrep[...] = jnp.full(mrep.shape, -jnp.inf, jnp.float32)

    def chunk(k, carry):
        pz = lax.rem(z + gray(k // NX), NZ) if NZ == 4 else lax.rem(z + k // NX, NZ)
        px = lax.rem(x + gray(lax.rem(k, NX)), NX) if NX == 4 else lax.rem(x + lax.rem(k, NX), NX)
        r = pz * NX + px

        @pl.when(k > 0)
        def _():
            part = tgt_all.at[r]
            pltpu.make_async_copy(part, part, tgt_recv.at[r]).wait()
        v = tgt_all[r, 0:D, :]
        norm = jnp.sum(v * v, axis=0, keepdims=True) * (-BITS)
        b = tgt_all[r, D:D + 1, :] * BITS + logb_ref[r] * LOG2E
        bias[r] = b
        hi, lo = split2(v)
        one = jnp.ones((1, TW), jnp.float32)
        tail = placed(D, [one] * 3 + list(split3(norm)) + list(split3(b)), TW)
        rhs = jnp.concatenate([hi, lo, hi, tail], axis=0).astype(jnp.bfloat16)

        def rows_of(i, c2):
            rows = pl.ds(pl.multiple_of(i * 128, 128), 128)
            t = jnp.dot(lhs[rows, :], rhs, preferred_element_type=jnp.float32)
            zs[r, rows, :] = t
            top = mrep[rows, :]
            for q in range(0, TW, 128):
                top = jnp.maximum(top, t[:, q:q + 128])
            mrep[rows, :] = top
            return c2
        lax.fori_loop(0, ROWS // 128, rows_of, 0)
        return carry
    lax.fori_loop(0, NR, chunk, 0)

    RB = 32
    diag = (lax.broadcasted_iota(jnp.int32, (128, 128), 0) == lax.broadcasted_iota(jnp.int32, (128, 128), 1))

    for it in range(ITERS):
        last = it == ITERS - 1

        def term(r):
            return delta[r] if it else None

        if it:
            def top_of(i, carry):
                rows = pl.ds(pl.multiple_of(i * RB, RB), RB)
                top = jnp.full((RB, 128), -jnp.inf, jnp.float32)
                for r in range(NR):
                    v = zs[r, rows, :] + delta[r]
                    for q in range(0, TW, 128):
                        top = jnp.maximum(top, v[:, q:q + 128])
                mrep[rows, :] = top
                return carry
            lax.fori_loop(0, ROWS // RB, top_of, 0)

        def sum_of(i, carry):
            rows = pl.ds(pl.multiple_of(i * RB, RB), RB)
            top = jnp.max(mrep[rows, :], axis=1, keepdims=True)
            acc = jnp.zeros((RB, 128), jnp.float32)
            for r in range(NR):
                v = zs[r, rows, :]
                if it:
                    v = v + delta[r]
                e = jnp.exp2(v - top)
                for q in range(0, TW, 128):
                    acc = acc + e[:, q:q + 128]
            mrep[rows, :] = jnp.broadcast_to(top, (RB, 128))
            sacc[rows, :] = acc
            return carry
        lax.fori_loop(0, ROWS // RB, sum_of, 0)

        packed = []
        for t in range(ROWS // 128):
            rows = slice(t * 128, (t + 1) * 128)
            s = jnp.sum(sacc[rows, :], axis=1, keepdims=True)
            part = mrep[rows, :] + jnp.log2(s)
            packed.append(jnp.sum(jnp.where(diag, part, 0.0), axis=0, keepdims=True))
        f_buf[it, col] = jnp.concatenate(packed, axis=0)
        to_all(col_peer, NK, lambda k: f_buf.at[it, col], f_buf.at[it, col], f_sems.at[it, 0], f_sems.at[it, 1])
        wait_bytes(f_buf.at[it], NK - 1, f_sems.at[it, 1])
        parts = f_buf[it]
        top = jnp.max(parts, axis=0)
        whole = top + jnp.log2(jnp.sum(jnp.exp2(parts - top[None]), axis=0))
        if last:
            f_ref[...] = whole * (-NATS)
        term_rows = loga_ref[...] * LOG2E - whole
        for t in range(ROWS // 128):
            v = jnp.where(diag, term_rows[t:t + 1, :], 0.0)
            s = jnp.sum(v, axis=1, keepdims=True)
            mrep[t * 128:(t + 1) * 128, :] = jnp.broadcast_to(s, (128, 128))

        def column(r, carry):
            def tops(i, acc):
                rows = pl.ds(pl.multiple_of(i * 128, 128), 128)
                f = mrep[rows, :]
                out = []
                for n, q in enumerate(range(0, TW, 128)):
                    v = zs[r, rows, q:q + 128] + f
                    out.append(jnp.maximum(acc[n], jnp.max(v.reshape(16, 8, 128), axis=0)))
                return tuple(out)
            low = tuple(jnp.full((8, 128), -jnp.inf, jnp.float32) for _ in range(0, TW, 128))
            tops_ = lax.fori_loop(0, ROWS // 128, tops, low)
            tops_ = [jnp.max(t, axis=0, keepdims=True) for t in tops_]

            def sums(i, acc):
                rows = pl.ds(pl.multiple_of(i * 128, 128), 128)
                f = mrep[rows, :]
                out = []
                for n, q in enumerate(range(0, TW, 128)):
                    v = jnp.exp2((zs[r, rows, q:q + 128] + f) - tops_[n])
                    out.append(acc[n] + jnp.sum(v.reshape(16, 8, 128), axis=0))
                return tuple(out)
            none = tuple(jnp.zeros((8, 128), jnp.float32) for _ in range(0, TW, 128))
            sums_ = lax.fori_loop(0, ROWS // 128, sums, none)
            sums_ = [jnp.sum(s, axis=0, keepdims=True) for s in sums_]
            val = jnp.concatenate([t + jnp.log2(s) for t, s in zip(tops_, sums_)], axis=1)
            c_send[it, r] = val - bias[r]
            return carry
        lax.fori_loop(0, NR, column, 0)
        c_buf[it, row] = c_send[it, row]
        to_all(
            row_peer, NR, lambda k: c_send.at[it, lax.rem(row + k, NR)], c_buf.at[it, row],
            c_sems.at[it, 0], c_sems.at[it, 1],
        )
        wait_bytes(c_buf.at[it], NR - 1, c_sems.at[it, 1])
        top = c_buf[it, 0]
        for r in range(1, NR):
            top = jnp.maximum(top, c_buf[it, r])
        tot = jnp.exp2(c_buf[it, 0] - top)
        for r in range(1, NR):
            tot = tot + jnp.exp2(c_buf[it, r] - top)
        mapped = (top + jnp.log2(tot)) * (-NATS)

        if it == 0:
            images = [hm_ref[k:k + 1, :] for k in range(HIST - 1)] + [mapped]
            base = [hg_ref[k:k + 1, :] for k in range(HIST - 1)] + [g_ref[...]]
        else:
            images = images[1:] + [mapped]
            base = base[1:] + [g_own]
        resid = placed(8, [p - q for p, q in zip(images, base)], TW)
        lane = lax.broadcasted_iota(jnp.int32, (8, 128), 1)
        sub = lax.broadcasted_iota(jnp.int32, (8, 128), 0)
        flat = jnp.zeros((8, 128), jnp.float32)
        for b in range(HIST):
            prod = jnp.sum(resid * resid[b:b + 1, :], axis=1, keepdims=True)
            flat = jnp.where(lane == sub * 8 + b, prod, flat)
        flat = jnp.sum(flat, axis=0, keepdims=True)
        m_buf[it, row, :, 0:TW] = mapped
        m_buf[it, row, :, TW:TW + 128] = flat
        to_all(row_peer, NR, lambda k: m_buf.at[it, row], m_buf.at[it, row], m_sems.at[it, 0], m_sems.at[it, 1])
        wait_bytes(m_buf.at[it], NR - 1, m_sems.at[it, 1])
        flat = m_buf[it, 0, :, TW:TW + 128]
        for r in range(1, NR):
            flat = flat + m_buf[it, r, :, TW:TW + 128]
        r_buf[it, col] = flat
        to_all(col_peer, NK, lambda k: r_buf.at[it, col], r_buf.at[it, col], r_sems.at[it, 0], r_sems.at[it, 1])
        wait_bytes(r_buf.at[it], NK - 1, r_sems.at[it, 1])
        flat = r_buf[it, 0]
        for b in range(1, NK):
            flat = flat + r_buf[it, b]
        line = lax.broadcasted_iota(jnp.int32, (1, 128), 1)
        gram = {
            (a, b): jnp.sum(jnp.where(line == a * 8 + b, flat, 0.0), axis=1, keepdims=True)
            for a in range(HIST) for b in range(a, HIST)
        }
        mix = solve(gram)
        g_own = images[0] * mix[0]
        for k in range(1, HIST):
            g_own = g_own + images[k] * mix[k]
        if last:
            gout_ref[...] = g_own
        else:
            def renew(r, carry):
                acc = m_buf[it, r, :, 0:TW] * mix[HIST - 1]
                for k in range(HIST - 1):
                    acc = acc + tgt_all[r, D + 1 + k:D + 2 + k, :] * mix[k]
                b = acc * BITS + logb_ref[r] * LOG2E
                delta[r] = b - bias[r]
                return carry
            lax.fori_loop(0, NR, renew, 0)

    wait_bytes(src_all, NK - 1, src_send)
    wait_bytes(tgt_all, NR - 1, tgt_send)
    for it in range(ITERS):
        wait_bytes(f_buf.at[it], NK - 1, f_sems.at[it, 0])
        wait_bytes(c_buf.at[it], NR - 1, c_sems.at[it, 0])
        wait_bytes(m_buf.at[it], NR - 1, m_sems.at[it, 0])
        wait_bytes(r_buf.at[it], NK - 1, r_sems.at[it, 0])


def shards(dims, src, tgt, log_a, log_b, g, hist_g, hist_maps):
    NZ, NX, NY, NC = dims
    NR, NK = NZ * NX, NY * NC
    D, SW = src.shape
    TW = tgt.shape[1]
    ROWS = NK * SW
    f32 = jnp.float32
    vmem = pl.BlockSpec(memory_space=pltpu.VMEM)
    dma = pltpu.SemaphoreType.DMA
    f, gout = pl.pallas_call(
        functools.partial(kernel, dims),
        out_shape=(
            jax.ShapeDtypeStruct((ROWS // 128, 128), f32),
            jax.ShapeDtypeStruct((1, TW), f32),
        ),
        in_specs=[vmem] * 7,
        out_specs=(vmem, vmem),
        scratch_shapes=[
            pltpu.VMEM((NR, D + 8, TW), f32),
            pltpu.VMEM((NK, D, SW), f32),
            pltpu.VMEM((ROWS, 4 * D), jnp.bfloat16),
            pltpu.VMEM((NR, ROWS, TW), f32),
            pltpu.VMEM((ROWS, 128), f32),
            pltpu.VMEM((ROWS, 128), f32),
            pltpu.VMEM((NR, 1, TW), f32),
            pltpu.VMEM((NR, 1, TW), f32),
            pltpu.VMEM((ITERS, NK, ROWS // 128, 128), f32),
            pltpu.VMEM((ITERS, NR, 1, TW), f32),
            pltpu.VMEM((ITERS, NR, 1, TW), f32),
            pltpu.VMEM((ITERS, NR, 1, TW + 128), f32),
            pltpu.VMEM((ITERS, NK, 1, 128), f32),
            dma, dma((NR,)), dma, dma,
            dma((ITERS, 2)), dma((ITERS, 2)), dma((ITERS, 2)), dma((ITERS, 2)),
        ],
        compiler_params=pltpu.CompilerParams(
            collective_id=0, has_side_effects=True, vmem_limit_bytes=48 * 1024 * 1024
        ),
        name="sinkhorn",
    )(src, tgt, log_a.reshape(ROWS // 128, 128), log_b.reshape(NR, 1, TW), g.reshape(1, TW), hist_g, hist_maps)
    return f.reshape(-1), gout.reshape(-1)


def solution(mesh, dims=(4, 4, 4, 2)):
    grid = Mesh(mesh.devices.reshape(dims), AXES)
    in_specs = (
        P(None, AXES),
        P(None, ("y", "core", "z", "x")),
        P(("z", "x")),
        P(("y", "core")),
        P(("y", "core", "z", "x")),
        P(None, ("y", "core", "z", "x")),
        P(None, ("y", "core", "z", "x")),
    )
    out_specs = (P(("z", "x")), P(("y", "core", "z", "x")))
    return jax.shard_map(
        functools.partial(shards, dims), mesh=grid, in_specs=in_specs, out_specs=out_specs, check_vma=False
    )
```

time: 336 us -> 112 us (0.33)
  Pallas kernels: 0 us -> 105 us
  blocking collectives: 102 us -> 0 us
  other arithmetic: 73.9 us -> 0 us
  between operations: 47.3 us -> 0.66 us
  waiting for transfers between devices: 30.8 us -> 0 us
  starting transfers between devices: 30 us -> 0 us
  local copies, waits for them, and re-layouts: 26.3 us -> 5.52 us
  matrix products: 17.7 us -> 0 us
  loops' own time: 5.46 us -> 0 us
    pallas_call x0 -> x1, Pallas kernels: none -> 105 us  [shards(): pl.pallas_call(functools.partial(kernel, dims), out_shape=(jax.ShapeDtype...]
    psum x8 -> x0, blocking collectives: 61.6 us -> none  [one_axis_at_a_time(): return functools.reduce(lax.psum, axes, array)]
    reduce_sum x14 -> x0, other arithmetic: 36.8 us -> none  [the longest x4 17.8 us: row_part(): return (top, jnp.sum(jnp.exp(scores - top[:, None]), axis=1))]
    reduce_max x10 -> x0, other arithmetic: 35.4 us -> none  [the longest x4 18.2 us: column_step(): top = jnp.max(scores, axis=0)]
    all_to_all x7 -> x0, waiting for transfers between devices: 30.8 us -> none  [the longest x6 25 us: from_everyone(): return lax.all_to_all(copies, axis, split_axis=0, concat_axis=0, tiled=True)]
    all_to_all x7 -> x0, starting transfers between devices: 30 us -> none  [the longest x6 26.5 us: from_everyone(): return lax.all_to_all(copies, axis, split_axis=0, concat_axis=0, tiled=True)]
    all_to_all x2 -> x0, blocking collectives: 25.2 us -> none  [the longest x1 14.7 us: from_everyone(): return lax.all_to_all(copies, axis, split_axis=0, concat_axis=0, tiled=True)]
    dot_general x5 -> x0, matrix products: 17.7 us -> none  [the longest x1 16.6 us: cost_of(): lax.dot_general(source, target, (((0,), (0,)), ((), ())), precision=lax.P...]
  transfers between devices with their start and end apart: 7 -> 0, of which waited for: 6 -> 0; matrix products, arithmetic and copies ran while one was open for 0% -> 0% of each run, Pallas kernels for 0% -> 0%
where the time goes in v1:
time: 112 us; the launch traced here: 111 us
  Pallas kernels  105 us (94%)
  local copies, waits for them, and re-layouts  5.52 us (5%)
    pallas_call x1, Pallas kernels, shards(): pl.pallas_call(functools.partial(kernel, dims), out_shape=(jax.ShapeDtype...  105 us
    unnamed x16, local copies, waits for them, and re-layouts  5.52 us

profile of v1, /device:TPU:1, one launch (start us, length us, event | category | flops | bytes accessed | tf_op | source)
XLA Modules:
  0.0 111.5 jit_solution(12832376476614342126)
XLA Ops:
  0.6 0.0 copy-start.3
  0.6 0.0 copy-start.6
  0.7 0.7 copy-done.3
  1.3 0.0 copy-done.6
  1.3 0.0 copy-start
  1.3 0.8 copy-done
  2.2 0.0 copy-start.1
  2.2 0.8 copy-done.1
  2.9 0.0 copy-start.2
  2.9 0.7 copy-done.2
  3.6 0.0 copy-start.4
  3.6 0.7 copy-done.4
  4.3 0.0 copy-start.5
  4.3 0.7 copy-done.5
  5.0 105.3 %sinkhorn.1 = (f32[8,128]{1,0:T(8,128)S(1)}, f32[1,256]{1,0:T(1,128)S(1)}) custom-call(f32[64,128]{1,0:T(8,128)S(1)} %copy-done.1, f32[64,256]{1,0:T(8,128)S(1)} %copy-done, f32[8,128]{1,0:T(8,128)S(1)} %bitcast.6, f32[16,1,256]{2,1,0:T(1,128)S(1)} %bitcast.5, f32[1,256]{1,0:T(1,128)S(1)} %bitcast.8, f32[4,256]{1,0:T(4,128)S(1)} %copy-done.4, ...), custom_call_target="tpu_custom_call" | custom-call | tf_op jit(solution)/shard_map/sinkhorn/pallas_call | solution.py:339
  110.3 0.6 copy.11
  110.9 0.6 copy.12
Async XLA Ops:
  0.6 0.7 copy-start.3
  0.6 0.7 copy-start.6
  1.3 0.8 copy-start
  2.2 0.8 copy-start.1
  2.9 0.7 copy-start.2
  3.6 0.7 copy-start.4
  4.3 0.7 copy-start.5

commit v2 on v1

--- a/solution.py
+++ b/solution.py
@@ -70,19 +70,21 @@
 
 def kernel(
     dims,
-    src_ref, tgt_ref, loga_ref, logb_ref, g_ref, hg_ref, hm_ref,
+    src_hbm, tgt_hbm, loga_hbm, logb_hbm, g_hbm, hg_hbm, hm_hbm,
     f_ref, gout_ref,
-    tgt_all, src_all, lhs, zs, mrep, sacc, bias, delta,
+    tgt_all, src_all, g_in, hm_in, loga_ref, logb_ref, hg_ref,
+    lhs, zs, mrep, sacc, bias, delta,
     f_buf, c_send, c_buf, m_buf, r_buf,
-    tgt_send, tgt_recv, src_send, src_recv, f_sems, c_sems, m_sems, r_sems,
+    in_sems, tgt_send, tgt_recv, src_send, src_recv, f_sems, c_sems, m_sems, r_sems,
 ):
     NZ, NX, NY, NC = dims
+    SIZE = dict(zip(AXES, dims))
     NR, NK = NZ * NX, NY * NC
-    D, SW = src_ref.shape
-    TW = tgt_ref.shape[1]
+    D, SW = src_hbm.shape
+    TW = tgt_hbm.shape[1]
     ROWS = NK * SW
-    z, x = lax.axis_index("z"), lax.axis_index("x")
-    y, core = lax.axis_index("y"), lax.axis_index("core")
+    at = {name: lax.axis_index(name) for name in AXES}
+    z, x, y, core = (at[name] for name in AXES)
     row, col = z * NX + x, y * NC + core
 
     def row_peer(k):
@@ -93,41 +95,116 @@
         p = lax.rem(col + k, NK)
         return {"y": p // NC, "core": lax.rem(p, NC)}
 
+    def near(axis, d):
+        return {axis: lax.rem(at[axis] + d + SIZE[axis], SIZE[axis])}
+
+    def remote(src, dst, ssem, rsem, peer):
+        pltpu.make_async_remote_copy(
+            src_ref=src, dst_ref=dst, send_sem=ssem, recv_sem=rsem, device_id=peer, device_id_type=MESH
+        ).start()
+
     def to_all(peer, count, src, dst, ssem, rsem):
         def one(k, carry):
-            pltpu.make_async_remote_copy(
-                src_ref=src(k), dst_ref=dst, send_sem=ssem, recv_sem=rsem,
-                device_id=peer(k), device_id_type=MESH,
-            ).start()
+            remote(src(k), dst, ssem, rsem, peer(k))
             return carry
         lax.fori_loop(1, count, one, 0)
 
     def wait_bytes(buf, count, sem):
-        part = buf.at[pl.ds(0, count)]
+        if count:
+            part = buf.at[pl.ds(0, count)]
+            pltpu.make_async_copy(part, part, sem).wait()
+
+    def wait_for(part, sem):
         pltpu.make_async_copy(part, part, sem).wait()
 
-    mine = tgt_all.at[row]
-    mine[0:D, :] = tgt_ref[...]
-    mine[D:D + 8, :] = placed(8, [g_ref[...]] + [hm_ref[k:k + 1, :] for k in range(HIST - 1)], TW)
-    src_all[col] = src_ref[...]
-
     barrier = pltpu.get_barrier_semaphore()
-
-    def greet(peer):
-        def one(k, carry):
-            pl.semaphore_signal(barrier, inc=1, device_id=peer(k), device_id_type=MESH)
-            return carry
-        return one
-    lax.fori_loop(1, NR, greet(row_peer), 0)
-    lax.fori_loop(1, NK, greet(col_peer), 0)
-    pl.semaphore_wait(barrier, NR + NK - 2)
-
-    to_all(col_peer, NK, lambda k: src_all.at[col], src_all.at[col], src_send, src_recv)
-    to_all(row_peer, NR, lambda k: tgt_all.at[row], tgt_all.at[row], tgt_send, tgt_recv.at[row])
-
-    wait_bytes(src_all, NK - 1, src_recv)
-
-    def left(b, carry):
+    around = [(name, d) for name in ("x", "z", "y") if SIZE[name] > 1 for d in (1, -1)]
+    if NC > 1:
+        around.append(("core", 1))
+    for name, d in around:
+        pl.semaphore_signal(barrier, inc=1, device_id=near(name, d), device_id_type=MESH)
+
+    moves = [
+        (tgt_hbm, tgt_all.at[row, pl.ds(0, D)]), (src_hbm, src_all.at[col]), (g_hbm, g_in), (logb_hbm, logb_ref),
+        (loga_hbm, loga_ref), (hm_hbm, hm_in), (hg_hbm, hg_ref),
+    ]
+    moves = [pltpu.make_async_copy(s, d, in_sems.at[k]) for k, (s, d) in enumerate(moves)]
+    for m in moves:
+        m.start()
+    mrep[...] = jnp.full(mrep.shape, -jnp.inf, jnp.float32)
+    for m in moves:
+        m.wait()
+    tgt_all[row, D:D + 8, :] = placed(8, [g_in[...]] + [hm_in[k:k + 1, :] for k in range(HIST - 1)], TW)
+    pl.semaphore_wait(barrier, len(around))
+
+    HALF = D // 2
+    QUART = D // 4
+    EXTRA = 8
+    PIECES = {
+        (0, None): (0, HALF), (0, 0): (0, QUART), (0, 1): (QUART, QUART),
+        (1, None): (HALF, HALF + EXTRA), (1, 0): (HALF, QUART + EXTRA), (1, 1): (HALF + QUART + EXTRA, QUART),
+    }
+    ORDER = (("x", "z"), ("z", "x"))
+
+    def slot(h, da, db):
+        a, b = ORDER[h]
+        d = {a: da, b: db}
+        return lax.rem(z + d["z"] + NZ, NZ) * NX + lax.rem(x + d["x"] + NX, NX)
+
+    def piece(r, h, sub=None):
+        start, count = PIECES[h, sub]
+        return tgt_all.at[r, pl.ds(start, count)]
+
+    def pass_on(r, h, sub, axis, d):
+        part = piece(r, h, sub)
+        remote(part, part, tgt_send, tgt_recv.at[h, r], near(axis, d))
+
+    def arrived(h, da, db):
+        a, b = ORDER[h]
+        if (da and SIZE[a] == 1) or (db and SIZE[b] == 1):
+            return
+        r = slot(h, da, db)
+        if da or db:
+            wait_for(piece(r, h), tgt_recv.at[h, r])
+        if db == 0:
+            if da == 0 and SIZE[a] > 1:
+                for d in (1, -1):
+                    pass_on(r, h, None, a, d)
+            elif da in (1, -1):
+                pass_on(r, h, 0 if da < 0 else 1, a, -da)
+            if SIZE[b] > 1:
+                for d in (1, -1):
+                    pass_on(r, h, None, b, d)
+        elif db in (1, -1):
+            pass_on(r, h, 0 if db < 0 else 1, b, -db)
+
+    def source(c, sub=None):
+        if sub is None:
+            return src_all.at[c]
+        return src_all.at[c, pl.ds(sub * HALF, HALF)]
+
+    def src_slot(dy, other=0):
+        return lax.rem(y + dy + NY, NY) * NC + lax.rem(core + other, NC)
+
+    def src_pass(c, sub, axis, d):
+        part = source(c, sub)
+        remote(part, part, src_send, src_recv.at[c], near(axis, d))
+
+    def src_arrived(dy):
+        if dy and NY == 1:
+            return
+        c = src_slot(dy)
+        if dy:
+            wait_for(source(c), src_recv.at[c])
+        if dy == 0 and NY > 1:
+            for d in (1, -1):
+                src_pass(c, None, "y", d)
+        elif dy in (1, -1):
+            src_pass(c, 0 if dy < 0 else 1, "y", -dy)
+        if NC > 1:
+            src_pass(c, None, "core", 1)
+
+    def left(b):
         v = src_all[b]
         norm = jnp.sum(v * v, axis=0, keepdims=True) * (-BITS)
         hi, lo = split2(v * (2.0 * BITS))
@@ -135,20 +212,10 @@
         tail = placed(D, list(split3(norm)) + [one] * 6, SW)
         full = jnp.concatenate([hi, hi, lo, tail], axis=0)
         lhs[pl.ds(pl.multiple_of(b * SW, SW), SW), :] = full.T.astype(jnp.bfloat16)
-        return carry
-    lax.fori_loop(0, NK, left, 0)
-
-    mrep[...] = jnp.full(mrep.shape, -jnp.inf, jnp.float32)
-
-    def chunk(k, carry):
-        pz = lax.rem(z + gray(k // NX), NZ) if NZ == 4 else lax.rem(z + k // NX, NZ)
-        px = lax.rem(x + gray(lax.rem(k, NX)), NX) if NX == 4 else lax.rem(x + lax.rem(k, NX), NX)
-        r = pz * NX + px
-
-        @pl.when(k > 0)
-        def _():
-            part = tgt_all.at[r]
-            pltpu.make_async_copy(part, part, tgt_recv.at[r]).wait()
+
+    MB = min(256, ROWS)
+
+    def chunk(r):
         v = tgt_all[r, 0:D, :]
         norm = jnp.sum(v * v, axis=0, keepdims=True) * (-BITS)
         b = tgt_all[r, D:D + 1, :] * BITS + logb_ref[r] * LOG2E
@@ -159,7 +226,7 @@
         rhs = jnp.concatenate([hi, lo, hi, tail], axis=0).astype(jnp.bfloat16)
 
         def rows_of(i, c2):
-            rows = pl.ds(pl.multiple_of(i * 128, 128), 128)
+            rows = pl.ds(pl.multiple_of(i * MB, MB), MB)
             t = jnp.dot(lhs[rows, :], rhs, preferred_element_type=jnp.float32)
             zs[r, rows, :] = t
             top = mrep[rows, :]
@@ -167,9 +234,78 @@
                 top = jnp.maximum(top, t[:, q:q + 128])
             mrep[rows, :] = top
             return c2
-        lax.fori_loop(0, ROWS // 128, rows_of, 0)
-        return carry
-    lax.fori_loop(0, NR, chunk, 0)
+        lax.fori_loop(0, ROWS // MB, rows_of, 0)
+
+    def chunks(count, offset):
+        def one(k, carry):
+            dz, dx = offset(k)
+            chunk(lax.rem(z + dz + NZ, NZ) * NX + lax.rem(x + dx + NX, NX))
+            return carry
+        lax.fori_loop(0, count, one, 0)
+
+    both = NZ > 1 and NX > 1
+    for h in (0, 1):
+        arrived(h, 0, 0)
+    src_arrived(0)
+    left(col)
+    for dy in (1, -1):
+        src_arrived(dy)
+    for h in (0, 1):
+        for da in (1, -1):
+            arrived(h, da, 0)
+    for h in (0, 1):
+        for db in (1, -1):
+            arrived(h, 0, db)
+    src_arrived(2)
+    if NY > 1:
+        for dy in (1, -1, 2):
+            left(src_slot(dy))
+    for h in (0, 1):
+        arrived(h, 2, 0)
+        for da in (1, -1):
+            for db in (1, -1):
+                arrived(h, da, db)
+    if NC > 1:
+        for dy in ((0, 1, -1, 2) if NY > 1 else (0,)):
+            c = src_slot(dy, 1)
+            wait_for(source(c), src_recv.at[c])
+            left(c)
+
+    def first(k):
+        i = jnp.maximum(k - 1, 0)
+        s = (1 - 2 * lax.rem(i, 2)) * jnp.minimum(k, 1)
+        return s * (i // 2), s * (1 - i // 2)
+    if both:
+        chunks(5, first)
+    elif NZ > 1:
+        chunks(3, lambda k: (lax.rem(k + 1, 3) - 1, 0))
+    elif NX > 1:
+        chunks(3, lambda k: (0, lax.rem(k + 1, 3) - 1))
+    else:
+        chunks(1, lambda k: (0, 0))
+    for h in (0, 1):
+        for db in (1, -1):
+            arrived(h, 2, db)
+        arrived(h, 0, 2)
+    if both:
+        chunks(4, lambda k: (1 - 2 * (k // 2), 1 - 2 * lax.rem(k, 2)))
+        chunks(2, lambda k: (2 * k, 2 - 2 * k))
+    elif NZ > 1:
+        chunks(1, lambda k: (2, 0))
+    elif NX > 1:
+        chunks(1, lambda k: (0, 2))
+    for h in (0, 1):
+        for da in (1, -1, 2):
+            arrived(h, da, 2)
+    if both:
+        chunks(2, lambda k: (2, 1 - 2 * k))
+        chunks(2, lambda k: (1 - 2 * k, 2))
+        chunks(1, lambda k: (2, 2))
+
+    def lane_tops():
+        for t in range(ROWS // 128):
+            rows = slice(t * 128, (t + 1) * 128)
+            mrep[rows, :] = jnp.broadcast_to(jnp.max(mrep[rows, :], axis=1, keepdims=True), (128, 128))
 
     RB = 32
     diag = (lax.broadcasted_iota(jnp.int32, (128, 128), 0) == lax.broadcasted_iota(jnp.int32, (128, 128), 1))
@@ -191,19 +327,18 @@
                 mrep[rows, :] = top
                 return carry
             lax.fori_loop(0, ROWS // RB, top_of, 0)
+        lane_tops()
 
         def sum_of(i, carry):
             rows = pl.ds(pl.multiple_of(i * RB, RB), RB)
-            top = jnp.max(mrep[rows, :], axis=1, keepdims=True)
+            top = mrep[rows, :]
             acc = jnp.zeros((RB, 128), jnp.float32)
             for r in range(NR):
                 v = zs[r, rows, :]
                 if it:
                     v = v + delta[r]
-                e = jnp.exp2(v - top)
                 for q in range(0, TW, 128):
-                    acc = acc + e[:, q:q + 128]
-            mrep[rows, :] = jnp.broadcast_to(top, (RB, 128))
+                    acc = acc + jnp.exp2(v[:, q:q + 128] - top)
             sacc[rows, :] = acc
             return carry
         lax.fori_loop(0, ROWS // RB, sum_of, 0)
@@ -271,8 +406,8 @@
         mapped = (top + jnp.log2(tot)) * (-NATS)
 
         if it == 0:
-            images = [hm_ref[k:k + 1, :] for k in range(HIST - 1)] + [mapped]
-            base = [hg_ref[k:k + 1, :] for k in range(HIST - 1)] + [g_ref[...]]
+            images = [hm_in[k:k + 1, :] for k in range(HIST - 1)] + [mapped]
+            base = [hg_ref[k:k + 1, :] for k in range(HIST - 1)] + [g_in[...]]
         else:
             images = images[1:] + [mapped]
             base = base[1:] + [g_own]
@@ -342,11 +477,16 @@
             jax.ShapeDtypeStruct((ROWS // 128, 128), f32),
             jax.ShapeDtypeStruct((1, TW), f32),
         ),
-        in_specs=[vmem] * 7,
+        in_specs=[pl.BlockSpec(memory_space=pltpu.HBM)] * 7,
         out_specs=(vmem, vmem),
         scratch_shapes=[
             pltpu.VMEM((NR, D + 8, TW), f32),
             pltpu.VMEM((NK, D, SW), f32),
+            pltpu.VMEM((1, TW), f32),
+            pltpu.VMEM((HIST - 1, TW), f32),
+            pltpu.VMEM((ROWS // 128, 128), f32),
+            pltpu.VMEM((NR, 1, TW), f32),
+            pltpu.VMEM((HIST - 1, TW), f32),
             pltpu.VMEM((ROWS, 4 * D), jnp.bfloat16),
             pltpu.VMEM((NR, ROWS, TW), f32),
             pltpu.VMEM((ROWS, 128), f32),
@@ -358,7 +498,7 @@
             pltpu.VMEM((ITERS, NR, 1, TW), f32),
             pltpu.VMEM((ITERS, NR, 1, TW + 128), f32),
             pltpu.VMEM((ITERS, NK, 1, 128), f32),
-            dma, dma((NR,)), dma, dma,
+            dma((7,)), dma, dma((2, NR)), dma, dma((NK,)),
             dma((ITERS, 2)), dma((ITERS, 2)), dma((ITERS, 2)), dma((ITERS, 2)),
         ],
         compiler_params=pltpu.CompilerParams(

time: 112 us -> 93.6 us (0.84)
  Pallas kernels: 105 us -> 87.1 us
    pallas_call x1, Pallas kernels: 105 us -> 87.1 us  [shards(): pl.pallas_call(functools.partial(kernel, dims), out_shape=(jax.ShapeDtype...]
where the time goes in v2:
time: 93.6 us; the launch traced here: 93.3 us
  Pallas kernels  87.1 us (93%)
  local copies, waits for them, and re-layouts  5.52 us (6%)
    pallas_call x1, Pallas kernels, shards(): pl.pallas_call(functools.partial(kernel, dims), out_shape=(jax.ShapeDtype...  87.1 us
    unnamed x16, local copies, waits for them, and re-layouts  5.52 us

profile of v2, /device:TPU:1, one launch (start us, length us, event | category | flops | bytes accessed | tf_op | source)
XLA Modules:
  0.0 93.3 jit_solution(4293973750661197608)
XLA Ops:
  0.6 0.0 copy-start.3
  0.6 0.0 copy-start.6
  0.7 0.7 copy-done.3
  1.3 0.0 copy-done.6
  1.3 0.0 copy-start
  1.3 0.8 copy-done
  2.2 0.0 copy-start.1
  2.2 0.8 copy-done.1
  2.9 0.0 copy-start.2
  2.9 0.7 copy-done.2
  3.6 0.0 copy-start.4
  3.6 0.7 copy-done.4
  4.3 0.0 copy-start.5
  4.3 0.7 copy-done.5
  5.0 87.1 %sinkhorn.1 = (f32[8,128]{1,0:T(8,128)S(1)}, f32[1,256]{1,0:T(1,128)S(1)}) custom-call(f32[64,128]{1,0:T(8,128)S(1)} %copy-done.1, f32[64,256]{1,0:T(8,128)S(1)} %copy-done, f32[8,128]{1,0:T(8,128)S(1)} %bitcast.6, f32[16,1,256]{2,1,0:T(1,128)S(1)} %bitcast.5, f32[1,256]{1,0:T(1,128)S(1)} %bitcast.8, f32[4,256]{1,0:T(4,128)S(1)} %copy-done.4, ...), custom_call_target="tpu_custom_call" | custom-call | tf_op jit(solution)/shard_map/sinkhorn/pallas_call | solution.py:474
  92.1 0.6 copy.11
  92.7 0.6 copy.12
Async XLA Ops:
  0.6 0.7 copy-start.3
  0.6 0.7 copy-start.6
  1.3 0.8 copy-start
  2.2 0.8 copy-start.1
  2.9 0.7 copy-start.2
  3.6 0.7 copy-start.4
  4.3 0.7 copy-start.5

commit v3 on v2

--- a/solution.py
+++ b/solution.py
@@ -14,6 +14,9 @@
 LOG2E = 1.4426950408889634
 BITS = LOG2E / EPS
 NATS = EPS / LOG2E
+FLAG_LANE = 63
+LEAST_BITS = -88.0
+SMALLEST = 2.0**LEAST_BITS
 MESH = pl.DeviceIdType.MESH
 AXES = ("z", "x", "y", "core")
 
@@ -69,11 +72,11 @@
 
 
 def kernel(
-    dims,
+    fast, dims,
     src_hbm, tgt_hbm, loga_hbm, logb_hbm, g_hbm, hg_hbm, hm_hbm,
-    f_ref, gout_ref,
+    f_ref, gout_ref, flag_ref,
     tgt_all, src_all, g_in, hm_in, loga_ref, logb_ref, hg_ref,
-    lhs, zs, mrep, sacc, bias, delta,
+    lhs, zs, mrep, sacc, m_rows, bias, delta,
     f_buf, c_send, c_buf, m_buf, r_buf,
     in_sems, tgt_send, tgt_recv, src_send, src_recv, f_sems, c_sems, m_sems, r_sems,
 ):
@@ -213,9 +216,7 @@
         full = jnp.concatenate([hi, hi, lo, tail], axis=0)
         lhs[pl.ds(pl.multiple_of(b * SW, SW), SW), :] = full.T.astype(jnp.bfloat16)
 
-    MB = min(256, ROWS)
-
-    def chunk(r):
+    def right(r):
         v = tgt_all[r, 0:D, :]
         norm = jnp.sum(v * v, axis=0, keepdims=True) * (-BITS)
         b = tgt_all[r, D:D + 1, :] * BITS + logb_ref[r] * LOG2E
@@ -223,23 +224,24 @@
         hi, lo = split2(v)
         one = jnp.ones((1, TW), jnp.float32)
         tail = placed(D, [one] * 3 + list(split3(norm)) + list(split3(b)), TW)
-        rhs = jnp.concatenate([hi, lo, hi, tail], axis=0).astype(jnp.bfloat16)
-
-        def rows_of(i, c2):
-            rows = pl.ds(pl.multiple_of(i * MB, MB), MB)
-            t = jnp.dot(lhs[rows, :], rhs, preferred_element_type=jnp.float32)
-            zs[r, rows, :] = t
-            top = mrep[rows, :]
-            for q in range(0, TW, 128):
-                top = jnp.maximum(top, t[:, q:q + 128])
-            mrep[rows, :] = top
-            return c2
-        lax.fori_loop(0, ROWS // MB, rows_of, 0)
-
-    def chunks(count, offset):
+        return jnp.concatenate([hi, lo, hi, tail], axis=0).astype(jnp.bfloat16)
+
+    def chunk(slots):
+        t = jnp.dot(
+            lhs[...], jnp.concatenate([right(r) for r in slots], axis=1), preferred_element_type=jnp.float32
+        )
+        top = mrep[...]
+        for n, r in enumerate(slots):
+            zs[r] = t[:, n * TW:(n + 1) * TW]
+        for q in range(0, len(slots) * TW, 128):
+            top = jnp.maximum(top, t[:, q:q + 128])
+        mrep[...] = top
+
+    def chunks(count, offsets):
         def one(k, carry):
-            dz, dx = offset(k)
-            chunk(lax.rem(z + dz + NZ, NZ) * NX + lax.rem(x + dx + NX, NX))
+            chunk([
+                lax.rem(z + dz + NZ, NZ) * NX + lax.rem(x + dx + NX, NX) for dz, dx in offsets(k)
+            ])
             return carry
         lax.fori_loop(0, count, one, 0)
 
@@ -271,43 +273,39 @@
             wait_for(source(c), src_recv.at[c])
             left(c)
 
-    def first(k):
-        i = jnp.maximum(k - 1, 0)
-        s = (1 - 2 * lax.rem(i, 2)) * jnp.minimum(k, 1)
-        return s * (i // 2), s * (1 - i // 2)
     if both:
-        chunks(5, first)
+        chunks(2, lambda k: ((k, 1 - k), (-k, k - 1)))
     elif NZ > 1:
-        chunks(3, lambda k: (lax.rem(k + 1, 3) - 1, 0))
+        chunks(1, lambda k: ((1, 0), (-1, 0)))
     elif NX > 1:
-        chunks(3, lambda k: (0, lax.rem(k + 1, 3) - 1))
+        chunks(1, lambda k: ((0, 1), (0, -1)))
     else:
-        chunks(1, lambda k: (0, 0))
+        chunks(1, lambda k: ((0, 0),))
     for h in (0, 1):
         for db in (1, -1):
             arrived(h, 2, db)
         arrived(h, 0, 2)
     if both:
-        chunks(4, lambda k: (1 - 2 * (k // 2), 1 - 2 * lax.rem(k, 2)))
-        chunks(2, lambda k: (2 * k, 2 - 2 * k))
+        chunks(2, lambda k: ((1, 1 - 2 * k), (-1, 1 - 2 * k)))
+        chunks(1, lambda k: ((2, 0), (0, 2)))
     elif NZ > 1:
-        chunks(1, lambda k: (2, 0))
+        chunks(1, lambda k: ((0, 0), (2, 0)))
     elif NX > 1:
-        chunks(1, lambda k: (0, 2))
+        chunks(1, lambda k: ((0, 0), (0, 2)))
     for h in (0, 1):
         for da in (1, -1, 2):
             arrived(h, da, 2)
     if both:
-        chunks(2, lambda k: (2, 1 - 2 * k))
-        chunks(2, lambda k: (1 - 2 * k, 2))
-        chunks(1, lambda k: (2, 2))
+        chunks(2, lambda k: ((2 - k, 3 * k - 1), (2 - 3 * k, 1 + k)))
+        chunks(1, lambda k: ((0, 0), (2, 2)))
 
     def lane_tops():
         for t in range(ROWS // 128):
             rows = slice(t * 128, (t + 1) * 128)
             mrep[rows, :] = jnp.broadcast_to(jnp.max(mrep[rows, :], axis=1, keepdims=True), (128, 128))
 
-    RB = 32
+    RB = min(32, ROWS)
+    bad = jnp.zeros((1, 1), jnp.float32)
     diag = (lax.broadcasted_iota(jnp.int32, (128, 128), 0) == lax.broadcasted_iota(jnp.int32, (128, 128), 1))
 
     for it in range(ITERS):
@@ -316,7 +314,8 @@
         def term(r):
             return delta[r] if it else None
 
-        if it:
+        shift = None
+        if it and not fast:
             def top_of(i, carry):
                 rows = pl.ds(pl.multiple_of(i * RB, RB), RB)
                 top = jnp.full((RB, 128), -jnp.inf, jnp.float32)
@@ -327,29 +326,54 @@
                 mrep[rows, :] = top
                 return carry
             lax.fori_loop(0, ROWS // RB, top_of, 0)
-        lane_tops()
+        if not (it and fast):
+            lane_tops()
+        if it and fast:
+            shift = jnp.max(jnp.concatenate([delta[r] for r in range(NR)], axis=0), axis=0, keepdims=True)
+            shift = jnp.max(shift, axis=1, keepdims=True)
+            for r in range(NR):
+                delta[r] = jnp.exp2(delta[r] - shift)
 
         def sum_of(i, carry):
             rows = pl.ds(pl.multiple_of(i * RB, RB), RB)
             top = mrep[rows, :]
             acc = jnp.zeros((RB, 128), jnp.float32)
             for r in range(NR):
-                v = zs[r, rows, :]
-                if it:
-                    v = v + delta[r]
                 for q in range(0, TW, 128):
-                    acc = acc + jnp.exp2(v[:, q:q + 128] - top)
+                    v = zs[r, rows, q:q + 128]
+                    if it and fast:
+                        acc = acc + v * delta[r, :, q:q + 128]
+                        continue
+                    if it:
+                        v = v + delta[r, :, q:q + 128]
+                    e = jnp.exp2(v - top)
+                    if fast:
+                        zs[r, rows, q:q + 128] = e
+                    acc = acc + e
             sacc[rows, :] = acc
             return carry
         lax.fori_loop(0, ROWS // RB, sum_of, 0)
 
         packed = []
+        least = None
         for t in range(ROWS // 128):
             rows = slice(t * 128, (t + 1) * 128)
             s = jnp.sum(sacc[rows, :], axis=1, keepdims=True)
             part = mrep[rows, :] + jnp.log2(s)
+            if it and fast:
+                part = part + shift
+                least = s if least is None else jnp.minimum(least, s)
             packed.append(jnp.sum(jnp.where(diag, part, 0.0), axis=0, keepdims=True))
         f_buf[it, col] = jnp.concatenate(packed, axis=0)
+        if it and fast:
+            bad = bad + jnp.max(jnp.where(least >= SMALLEST, 0.0, 1.0), axis=0, keepdims=True)
+        if fast:
+            if it == 0:
+                tops = [
+                    jnp.sum(jnp.where(diag, mrep[t * 128:(t + 1) * 128, :], 0.0), axis=0, keepdims=True)
+                    for t in range(ROWS // 128)
+                ]
+                m_rows[...] = jnp.concatenate(tops, axis=0)
         to_all(col_peer, NK, lambda k: f_buf.at[it, col], f_buf.at[it, col], f_sems.at[it, 0], f_sems.at[it, 1])
         wait_bytes(f_buf.at[it], NK - 1, f_sems.at[it, 1])
         parts = f_buf[it]
@@ -358,10 +382,38 @@
         if last:
             f_ref[...] = whole * (-NATS)
         term_rows = loga_ref[...] * LOG2E - whole
+        level = jnp.zeros((1, 1), jnp.float32)
+        if fast:
+            term_rows = term_rows + m_rows[...]
+            level = jnp.max(jnp.max(term_rows, axis=0, keepdims=True), axis=1, keepdims=True)
+            term_rows = jnp.exp2(term_rows - level)
+        weights = sacc if fast else mrep
         for t in range(ROWS // 128):
             v = jnp.where(diag, term_rows[t:t + 1, :], 0.0)
             s = jnp.sum(v, axis=1, keepdims=True)
-            mrep[t * 128:(t + 1) * 128, :] = jnp.broadcast_to(s, (128, 128))
+            weights[t * 128:(t + 1) * 128, :] = jnp.broadcast_to(s, (128, 128))
+
+        CB = min(4, NR)
+
+        def columns(i, carry):
+            slots = [i * CB + n for n in range(CB)]
+
+            def sums(k, acc):
+                rows = pl.ds(pl.multiple_of(k * 128, 128), 128)
+                u = weights[rows, :]
+                out = []
+                for n, r in enumerate(slots):
+                    for q in range(0, TW, 128):
+                        v = zs[r, rows, q:q + 128] * u
+                        out.append(acc[len(out)] + jnp.sum(v.reshape(16, 8, 128), axis=0))
+                return tuple(out)
+            none = tuple(jnp.zeros((8, 128), jnp.float32) for _ in range(CB * TW // 128))
+            found = lax.fori_loop(0, ROWS // 128, sums, none)
+            for n, r in enumerate(slots):
+                part = [jnp.sum(v, axis=0, keepdims=True) for v in found[n * TW // 128:(n + 1) * TW // 128]]
+                c_send[it, r, :, 0:TW] = jnp.log2(jnp.concatenate(part, axis=1)) + level - bias[r]
+                c_send[it, r, :, TW:TW + 128] = jnp.broadcast_to(level, (1, 128))
+            return carry
 
         def column(r, carry):
             def tops(i, acc):
@@ -388,22 +440,28 @@
             sums_ = lax.fori_loop(0, ROWS // 128, sums, none)
             sums_ = [jnp.sum(s, axis=0, keepdims=True) for s in sums_]
             val = jnp.concatenate([t + jnp.log2(s) for t, s in zip(tops_, sums_)], axis=1)
-            c_send[it, r] = val - bias[r]
+            c_send[it, r, :, 0:TW] = val - bias[r]
+            c_send[it, r, :, TW:TW + 128] = jnp.zeros((1, 128), jnp.float32)
             return carry
-        lax.fori_loop(0, NR, column, 0)
+        if fast:
+            lax.fori_loop(0, NR // CB, columns, 0)
+        else:
+            lax.fori_loop(0, NR, column, 0)
         c_buf[it, row] = c_send[it, row]
         to_all(
             row_peer, NR, lambda k: c_send.at[it, lax.rem(row + k, NR)], c_buf.at[it, row],
             c_sems.at[it, 0], c_sems.at[it, 1],
         )
         wait_bytes(c_buf.at[it], NR - 1, c_sems.at[it, 1])
-        top = c_buf[it, 0]
-        for r in range(1, NR):
-            top = jnp.maximum(top, c_buf[it, r])
-        tot = jnp.exp2(c_buf[it, 0] - top)
-        for r in range(1, NR):
-            tot = tot + jnp.exp2(c_buf[it, r] - top)
-        mapped = (top + jnp.log2(tot)) * (-NATS)
+        got = [c_buf[it, r, :, 0:TW] for r in range(NR)]
+        top = functools.reduce(jnp.maximum, got)
+        tot = functools.reduce(jnp.add, [jnp.exp2(v - top) for v in got])
+        mapped = top + jnp.log2(tot)
+        if fast:
+            levels = functools.reduce(jnp.maximum, [c_buf[it, r, :, TW:TW + 128] for r in range(NR)])
+            size = mapped + bias[row] - jnp.concatenate([levels] * (TW // 128), axis=1)
+            bad = bad + jnp.max(jnp.where(size >= LEAST_BITS, 0.0, 1.0), axis=1, keepdims=True)
+        mapped = mapped * (-NATS)
 
         if it == 0:
             images = [hm_in[k:k + 1, :] for k in range(HIST - 1)] + [mapped]
@@ -419,6 +477,8 @@
             prod = jnp.sum(resid * resid[b:b + 1, :], axis=1, keepdims=True)
             flat = jnp.where(lane == sub * 8 + b, prod, flat)
         flat = jnp.sum(flat, axis=0, keepdims=True)
+        line = lax.broadcasted_iota(jnp.int32, (1, 128), 1)
+        flat = jnp.where(line == FLAG_LANE, bad, flat)
         m_buf[it, row, :, 0:TW] = mapped
         m_buf[it, row, :, TW:TW + 128] = flat
         to_all(row_peer, NR, lambda k: m_buf.at[it, row], m_buf.at[it, row], m_sems.at[it, 0], m_sems.at[it, 1])
@@ -432,7 +492,6 @@
         flat = r_buf[it, 0]
         for b in range(1, NK):
             flat = flat + r_buf[it, b]
-        line = lax.broadcasted_iota(jnp.int32, (1, 128), 1)
         gram = {
             (a, b): jnp.sum(jnp.where(line == a * 8 + b, flat, 0.0), axis=1, keepdims=True)
             for a in range(HIST) for b in range(a, HIST)
@@ -443,6 +502,9 @@
             g_own = g_own + images[k] * mix[k]
         if last:
             gout_ref[...] = g_own
+            flag_ref[...] = jnp.broadcast_to(
+                jnp.sum(jnp.where(line == FLAG_LANE, flat, 0.0), axis=1, keepdims=True), (1, 128)
+            )
         else:
             def renew(r, carry):
                 acc = m_buf[it, r, :, 0:TW] * mix[HIST - 1]
@@ -471,14 +533,16 @@
     f32 = jnp.float32
     vmem = pl.BlockSpec(memory_space=pltpu.VMEM)
     dma = pltpu.SemaphoreType.DMA
-    f, gout = pl.pallas_call(
-        functools.partial(kernel, dims),
+    def call(fast):
+        return pl.pallas_call(
+        functools.partial(kernel, fast, dims),
         out_shape=(
             jax.ShapeDtypeStruct((ROWS // 128, 128), f32),
             jax.ShapeDtypeStruct((1, TW), f32),
+            jax.ShapeDtypeStruct((1, 128), f32),
         ),
         in_specs=[pl.BlockSpec(memory_space=pltpu.HBM)] * 7,
-        out_specs=(vmem, vmem),
+        out_specs=(vmem, vmem, vmem),
         scratch_shapes=[
             pltpu.VMEM((NR, D + 8, TW), f32),
             pltpu.VMEM((NK, D, SW), f32),
@@ -491,21 +555,25 @@
             pltpu.VMEM((NR, ROWS, TW), f32),
             pltpu.VMEM((ROWS, 128), f32),
             pltpu.VMEM((ROWS, 128), f32),
+            pltpu.VMEM((ROWS // 128, 128), f32),
             pltpu.VMEM((NR, 1, TW), f32),
             pltpu.VMEM((NR, 1, TW), f32),
             pltpu.VMEM((ITERS, NK, ROWS // 128, 128), f32),
-            pltpu.VMEM((ITERS, NR, 1, TW), f32),
-            pltpu.VMEM((ITERS, NR, 1, TW), f32),
+            pltpu.VMEM((ITERS, NR, 1, TW + 128), f32),
+            pltpu.VMEM((ITERS, NR, 1, TW + 128), f32),
             pltpu.VMEM((ITERS, NR, 1, TW + 128), f32),
             pltpu.VMEM((ITERS, NK, 1, 128), f32),
             dma((7,)), dma, dma((2, NR)), dma, dma((NK,)),
             dma((ITERS, 2)), dma((ITERS, 2)), dma((ITERS, 2)), dma((ITERS, 2)),
         ],
         compiler_params=pltpu.CompilerParams(
-            collective_id=0, has_side_effects=True, vmem_limit_bytes=48 * 1024 * 1024
+            collective_id=0 if fast else 1, has_side_effects=True, vmem_limit_bytes=48 * 1024 * 1024
         ),
-        name="sinkhorn",
+        name="sinkhorn" if fast else "sinkhorn_wide",
     )(src, tgt, log_a.reshape(ROWS // 128, 128), log_b.reshape(NR, 1, TW), g.reshape(1, TW), hist_g, hist_maps)
+
+    f, gout, flag = call(True)
+    f, gout = lax.cond(flag[0, 0] > 0.5, lambda: call(False)[:2], lambda: (f, gout))
     return f.reshape(-1), gout.reshape(-1)
 
 

time: 93.6 us -> 148 us (1.58)
  Pallas kernels: 87.1 us -> 145 us
  local copies, waits for them, and re-layouts: 5.52 us -> 2.47 us
    pallas_call x1 -> x2, Pallas kernels: 87.1 us -> 145 us  [call(): pl.pallas_call(functools.partial(kernel, fast, dims), out_shape=(jax.Shap...]
    unnamed x16, local copies, waits for them, and re-layouts: 5.52 us -> 2.47 us
where the time goes in v3:
time: 148 us
  Pallas kernels  145 us (98%)
  local copies, waits for them, and re-layouts  2.47 us (2%)
    pallas_call x2, Pallas kernels, call(): pl.pallas_call(functools.partial(kernel, fast, dims), out_shape=(jax.Shap...  145 us

profile of v3, /device:TPU:1, one launch (start us, length us, event | category | flops | bytes accessed | tf_op | source)
XLA Modules:
  0.0 147.8 jit_solution(1879330800475156322)
XLA Ops:
  0.6 0.0 copy-start.3
  0.6 0.0 copy-start.6
  0.7 0.7 copy-done.3
  1.3 0.0 copy-done.6
  1.3 0.0 copy-start
  1.3 0.0 copy-start.1
  1.3 0.0 copy-start.2
  1.3 67.5 %sinkhorn.1 = (f32[8,128]{1,0:T(8,128)S(1)}, f32[1,256]{1,0:T(1,128)S(1)}, f32[1,128]{1,0:T(1,128)S(1)}) custom-call(f32[64,128]{1,0:T(8,128)} %src_hbm.1, f32[64,256]{1,0:T(8,128)} %tgt_hbm.1, f32[8,128]{1,0:T(8,128)S(1)} %bitcast.15, f32[16,1,256]{2,1,0:T(1,128)} %bitcast.13, f32[1,256]{1,0:T(1,128)S(1)} %bitcast.17, f32[4,256]{1,0:T(4,128)} %hg_hbm.1, ...), custom_call_target="tpu_custom_call" | custom-call | tf_op jit(solution)/shard_map/sinkhorn/pallas_call | solution.py:537
  68.8 0.0 copy-start.5
  68.8 0.0 copy-start.4
  68.9 0.0 copy-done
  68.9 0.0 copy-done.1
  68.9 0.0 copy-done.2
  68.9 0.6 copy-done.5
  69.5 0.0 copy-done.4
  69.5 77.2 %conditional.1 = (f32[1024]{0:T(1024)S(1)}, f32[256]{0:T(256)S(1)}) conditional(s32[]{:T(128)} %bitcast.10, (f32[8,128]{1,0:T(8,128)S(1)}, f32[1,256]{1,0:T(1,128)S(1)}) %tuple.30, (f32[1024]{0:T(1024)S(1)}, f32[4096]{0:T(1024)S(1)}, f32[256]{0:T(256)S(1)}, f32[64,128]{1,0:T(8,128)S(1)}, f32[64,256]{1,0:T(8,128)S(1)}, ...), branch_computations={%region_0.0_spmd, %region_1.0_spmd} | conditional | bytes 16 | solution.py:576
  69.5 77.2 %sinkhorn_wide.1 = (f32[8,128]{1,0:T(8,128)S(1)}, f32[1,256]{1,0:T(1,128)S(1)}, f32[1,128]{1,0:T(1,128)}) custom-call(f32[64,128]{1,0:T(8,128)S(1)} %get-tuple-element.24.src_hbm, f32[64,256]{1,0:T(8,128)S(1)} %get-tuple-element.25.tgt_hbm, f32[8,128]{1,0:T(8,128)S(1)} %bitcast.16, f32[16,1,256]{2,1,0:T(1,128)S(1)} %bitcast.14, f32[1,256]{1,0:T(1,128)S(1)} %bitcast.18, ...), custom_call_target="tpu_custom_call" | custom-call | tf_op jit(solution)/shard_map/cond/branch_1_fun/sinkhorn_wide/pallas_call | solution.py:537
  146.7 0.6 copy.17
  147.3 0.6 copy.18
Async XLA Ops:
  0.6 0.7 copy-start.3
  0.6 0.7 copy-start.6
  1.3 67.5 %copy-start = (f32[64,256]{1,0:T(8,128)S(1)}, f32[64,256]{1,0:T(8,128)}, u32[]{:S(2)}) copy-start(f32[64,256]{1,0:T(8,128)} %tgt_hbm.1) | copy-start | bytes 196612
  1.3 67.5 %copy-start.1 = (f32[64,128]{1,0:T(8,128)S(1)}, f32[64,128]{1,0:T(8,128)}, u32[]{:S(2)}) copy-start(f32[64,128]{1,0:T(8,128)} %src_hbm.1) | copy-start | bytes 98308
  1.3 67.6 %copy-start.2 = (f32[4096]{0:T(1024)S(1)}, f32[4096]{0:T(1024)}, u32[]{:S(2)}) copy-start(f32[4096]{0:T(1024)} %param.12) | copy-start | bytes 49156
  68.8 0.7 copy-start.5
  68.8 0.7 copy-start.4

commit v4 on v2

v4 whole, which is shorter than its diff:
```python
import functools

import jax
import jax.numpy as jnp
from jax import lax
from jax.experimental import pallas as pl
from jax.experimental.pallas import tpu as pltpu
from jax.sharding import Mesh
from jax.sharding import PartitionSpec as P

HIST = 5
ITERS = 2
EPS = 0.1
LOG2E = 1.4426950408889634
BITS = LOG2E / EPS
NATS = EPS / LOG2E
LEAST_BITS = -97.0
SMALLEST = 2.0**LEAST_BITS
MESH = pl.DeviceIdType.MESH
AXES = ("z", "x", "y", "core")


def split2(v):
    hi = v.astype(jnp.bfloat16).astype(jnp.float32)
    return hi, v - hi


def split3(v):
    hi = v.astype(jnp.bfloat16).astype(jnp.float32)
    rest = v - hi
    mid = rest.astype(jnp.bfloat16).astype(jnp.float32)
    return hi, mid, rest - mid


def placed(rows, values, width):
    at = lax.broadcasted_iota(jnp.int32, (rows, width), 0)
    out = jnp.zeros((rows, width), jnp.float32)
    for k, v in enumerate(values):
        out = jnp.where(at == k, v, out)
    return out


def solve(gram):
    n = HIST
    trace = gram[0, 0]
    for k in range(1, n):
        trace = trace + gram[k, k]
    shift = 0.001 * trace / n + 1e-6
    a = [[gram[min(p, q), max(p, q)] + (shift if p == q else 0.0) for q in range(n)] for p in range(n)]
    rhs = [jnp.ones((1, 1), jnp.float32) for _ in range(n)]
    for p in range(n):
        for low in range(p + 1, n):
            factor = a[low][p] / a[p][p]
            for q in range(p + 1, n):
                a[low][q] = a[low][q] - factor * a[p][q]
            rhs[low] = rhs[low] - factor * rhs[p]
    out = [None] * n
    for p in reversed(range(n)):
        acc = rhs[p]
        for q in range(p + 1, n):
            acc = acc - a[p][q] * out[q]
        out[p] = acc / a[p][p]
    total = out[0]
    for k in range(1, n):
        total = total + out[k]
    return [o / total for o in out]


def kernel(
    fast, dims,
    src_hbm, tgt_hbm, loga_hbm, logb_hbm, g_hbm, hg_hbm, hm_hbm,
    f_ref, gout_ref, flag_ref,
    src_all, tgt_all, loga_in, logb_in, g_in, hg_in, hm_in,
    left, zs, wacc, vrep, hist, m_rows, a_rows, u_rows, g_tmp,
    f_buf, fo_buf, c_buf, r_buf,
    in_sems, src_send, src_recv, tgt_send, tgt_recv, f_sems, fo_sems, c_sems, r_sems,
):
    NZ, NX, NY, NC = dims
    SIZE = dict(zip(AXES, dims))
    NR, NK = NZ * NX, NY * NC
    D, SW = src_hbm.shape
    TW = tgt_hbm.shape[1]
    COLS = NK * TW
    NT = COLS // 128
    at = {name: lax.axis_index(name) for name in AXES}
    z, x, y, core = (at[name] for name in AXES)
    row, col = z * NX + x, y * NC + core

    def row_peer(k):
        p = lax.rem(row + k, NR)
        return {"z": p // NX, "x": lax.rem(p, NX)}

    def col_peer(k):
        p = lax.rem(col + k, NK)
        return {"y": p // NC, "core": lax.rem(p, NC)}

    def near(axis, d):
        return {axis: lax.rem(at[axis] + d + SIZE[axis], SIZE[axis])}

    def remote(part, ssem, rsem, peer):
        pltpu.make_async_remote_copy(
            src_ref=part, dst_ref=part, send_sem=ssem, recv_sem=rsem, device_id=peer, device_id_type=MESH
        ).start()

    def to_all(peer, count, part, sems):
        def one(k, carry):
            remote(part, sems.at[0], sems.at[1], peer(k))
            return carry
        lax.fori_loop(1, count, one, 0)

    def wait_for(part, sem):
        pltpu.make_async_copy(part, part, sem).wait()

    def wait_bytes(buf, count, sem):
        if count:
            wait_for(buf.at[pl.ds(0, count)], sem)

    barrier = pltpu.get_barrier_semaphore()
    around = [(name, d) for name in ("x", "z", "y") if SIZE[name] > 1 for d in (1, -1)]
    if NC > 1:
        around.append(("core", 1))
    for name, d in around:
        pl.semaphore_signal(barrier, inc=1, device_id=near(name, d), device_id_type=MESH)

    moves = [
        (src_hbm, src_all.at[row, pl.ds(0, D)]), (tgt_hbm, tgt_all.at[col, pl.ds(0, D)]), (loga_hbm, loga_in),
        (logb_hbm.at[row], logb_in), (g_hbm, g_in), (hm_hbm, hm_in), (hg_hbm, hg_in),
    ]
    moves = [pltpu.make_async_copy(s, d, in_sems.at[k]) for k, (s, d) in enumerate(moves)]
    for m in moves:
        m.start()
    for m in moves:
        m.wait()
    KEPT = HIST - 1
    src_all[row, D:D + 8, :] = placed(8, [loga_in[pl.ds(col, 1), :]], SW)
    tgt_all[col, D:D + 16, :] = placed(
        16, [g_in[...], logb_in[...]] + [hm_in[k:k + 1, :] for k in range(KEPT)]
        + [hg_in[k:k + 1, :] for k in range(KEPT)], TW
    )
    pl.semaphore_wait(barrier, len(around))

    HALF, QUART, EXTRA = D // 2, D // 4, 8
    PIECES = {
        (0, None): (0, HALF), (0, 0): (0, QUART), (0, 1): (QUART, QUART),
        (1, None): (HALF, HALF + EXTRA), (1, 0): (HALF, QUART + EXTRA), (1, 1): (HALF + QUART + EXTRA, QUART),
    }
    ORDER = (("x", "z"), ("z", "x"))

    def slot_of(dz, dx):
        return lax.rem(z + dz + NZ, NZ) * NX + lax.rem(x + dx + NX, NX)

    def piece(r, h, sub=None):
        start, count = PIECES[h, sub]
        return src_all.at[r, pl.ds(start, count)]

    def pass_on(r, h, sub, axis, d):
        remote(piece(r, h, sub), src_send, src_recv.at[h, r], near(axis, d))

    def arrived(h, da, db):
        a, b = ORDER[h]
        if (da and SIZE[a] == 1) or (db and SIZE[b] == 1):
            return
        r = slot_of(**{"d" + a: da, "d" + b: db})
        if da or db:
            wait_for(piece(r, h), src_recv.at[h, r])
        if db == 0:
            if da == 0 and SIZE[a] > 1:
                for d in (1, -1):
                    pass_on(r, h, None, a, d)
            elif da in (1, -1):
                pass_on(r, h, 0 if da < 0 else 1, a, -da)
            if SIZE[b] > 1:
                for d in (1, -1):
                    pass_on(r, h, None, b, d)
        elif db in (1, -1):
            pass_on(r, h, 0 if db < 0 else 1, b, -db)

    TROWS = D + 16

    def target(c, sub=None):
        if sub is None:
            return tgt_all.at[c]
        return tgt_all.at[c, pl.ds(sub * (TROWS // 2), TROWS // 2)]

    def tgt_slot(dy, other=0):
        return lax.rem(y + dy + NY, NY) * NC + lax.rem(core + other, NC)

    def tgt_pass(c, sub, axis, d):
        remote(target(c, sub), tgt_send, tgt_recv.at[c], near(axis, d))

    def tgt_arrived(dy):
        if dy and NY == 1:
            return
        c = tgt_slot(dy)
        if dy:
            wait_for(target(c), tgt_recv.at[c])
        if dy == 0 and NY > 1:
            for d in (1, -1):
                tgt_pass(c, None, "y", d)
        elif dy in (1, -1):
            tgt_pass(c, 0 if dy < 0 else 1, "y", -dy)
        if NC > 1:
            tgt_pass(c, None, "core", 1)

    def take_targets(c):
        v = tgt_all[c, 0:D, :]
        norm = jnp.sum(v * v, axis=0, keepdims=True) * (-BITS)
        b = tgt_all[c, D:D + 1, :] * BITS + tgt_all[c, D + 1:D + 2, :] * LOG2E
        hi, lo = split2(v)
        one = jnp.ones((1, TW), jnp.float32)
        tail = placed(D, list(split3(norm)) + list(split3(b)) + [one] * 3, TW)
        full = jnp.concatenate([hi, lo, hi, tail], axis=0)
        left[pl.ds(pl.multiple_of(c * TW, TW), TW), :] = full.T.astype(jnp.bfloat16)

    def sources(r):
        v = src_all[r, 0:D, :]
        norm = jnp.sum(v * v, axis=0, keepdims=True) * (-BITS)
        hi, lo = split2(v * (2.0 * BITS))
        one = jnp.ones((1, SW), jnp.float32)
        tail = placed(D, [one] * 6 + list(split3(norm)), SW)
        return jnp.concatenate([hi, hi, lo, tail], axis=0).astype(jnp.bfloat16)

    EB = min(256, COLS)

    def block(offsets):
        spots = [(lax.rem(z + dz + NZ, NZ), lax.rem(x + dx + NX, NX)) for dz, dx in offsets]
        slots = [zb * NX + xb for zb, xb in spots]
        t = jnp.dot(
            left[...], jnp.concatenate([sources(r) for r in slots], axis=1), preferred_element_type=jnp.float32
        )
        tops = []
        for n, r in enumerate(slots):
            part = t[:, n * SW:(n + 1) * SW]
            zs[r] = part
            tops.append(jnp.max(jnp.max(part.reshape(COLS // 8, 8, SW), axis=0), axis=0, keepdims=True))

        def expo(i, acc):
            rows = pl.ds(pl.multiple_of(i * EB, EB), EB)
            out = []
            for n, r in enumerate(slots):
                e = jnp.exp2(zs[r, rows, :] - tops[n])
                if fast:
                    zs[r, rows, :] = e
                out.append(acc[n] + jnp.sum(e.reshape(EB // 8, 8, SW), axis=0))
            return tuple(out)
        found = lax.fori_loop(0, COLS // EB, expo, tuple(jnp.zeros((8, SW), jnp.float32) for _ in slots))
        for n, (zb, xb) in enumerate(spots):
            f_buf[0, row, zb, pl.ds(xb, 1), :] = tops[n] + jnp.log2(jnp.sum(found[n], axis=0, keepdims=True))
            m_rows[zb, pl.ds(xb, 1), :] = tops[n]
            a_rows[zb, pl.ds(xb, 1), :] = src_all[slots[n], D:D + 1, :] * LOG2E

    def blocks(count, offsets):
        def one(k, carry):
            block(offsets(k))
            return carry
        lax.fori_loop(0, count, one, 0)

    def send_f(it, zb):
        to_all(row_peer, NR, f_buf.at[it, row, zb], f_sems.at[it])

    both = NZ > 1 and NX > 1
    tgt_arrived(0)
    for h in (0, 1):
        arrived(h, 0, 0)
    take_targets(col)
    for dy in (1, -1):
        tgt_arrived(dy)
    for h in (0, 1):
        for da in (1, -1):
            arrived(h, da, 0)
    for h in (0, 1):
        for db in (1, -1):
            arrived(h, 0, db)
    tgt_arrived(2)
    if NY > 1:
        for dy in (1, -1, 2):
            take_targets(tgt_slot(dy))
    for h in (0, 1):
        arrived(h, 2, 0)
        for da in (1, -1):
            for db in (1, -1):
                arrived(h, da, db)
    if NC > 1:
        for dy in ((0, 1, -1, 2) if NY > 1 else (0,)):
            c = tgt_slot(dy, 1)
            wait_for(target(c), tgt_recv.at[c])
            take_targets(c)
    if both:
        blocks(2, lambda k: ((k, 1 - k), (-k, k - 1)))
    for h in (0, 1):
        for db in (1, -1):
            arrived(h, 2, db)
        arrived(h, 0, 2)
    if both:
        blocks(2, lambda k: ((1, 1 - 2 * k), (-1, 1 - 2 * k)))
    block(((0, 0), (0, 2)) if both else ((0, 0),))
    for h in (0, 1):
        for da in (1, -1, 2):
            arrived(h, da, 2)
    send_f(0, z)
    if both:
        blocks(1, lambda k: ((1, 2), (-1, 2)))
        for d in (1, 3):
            send_f(0, lax.rem(z + d, NZ))
        blocks(2, lambda k: ((2, 1 - k), (2, 3 * k - 1)))
        send_f(0, lax.rem(z + 2, NZ))
    for c in range(NK):
        for k in range(2 * KEPT + 2):
            for q in range(TW // 128):
                t = c * (TW // 128) + q
                hist[k, t:t + 1, :] = tgt_all[c, D + k:D + k + 1, q * 128:(q + 1) * 128]

    bad = jnp.zeros((1, 1), jnp.float32)
    g_now = hist[0]
    bias = g_now * BITS + hist[1] * LOG2E
    images = [hist[2 + k] for k in range(KEPT)]
    base = [hist[2 + KEPT + k] for k in range(KEPT)]
    shift = jnp.zeros((1, 1), jnp.float32)
    pairs = [(a, b) for a in range(HIST) for b in range(a, HIST)]
    line = lax.broadcasted_iota(jnp.int32, (1, 128), 1)
    eye = (lax.broadcasted_iota(jnp.int32, (16, 128), 0) == lax.broadcasted_iota(jnp.int32, (16, 128), 1))

    def all_of(v, op):
        return op(op(v, axis=0, keepdims=True), axis=1, keepdims=True)

    def low(v):
        return all_of(jnp.where(v >= SMALLEST, 0.0, 1.0), jnp.max)

    for it in range(ITERS):
        last = it == ITERS - 1
        if it and fast:
            GZ = min(2, NZ)
            SB = min(128, COLS)
            for zg in range(0, NZ, GZ):
                spots = [(zz, xx) for zz in range(zg, zg + GZ) for xx in range(NX)]

                def weigh(i, acc):
                    rows = pl.ds(pl.multiple_of(i * SB, SB), SB)
                    v = vrep[rows, :]
                    return tuple(
                        a + jnp.sum((zs[zz * NX + xx, rows, :] * v).reshape(SB // 8, 8, SW), axis=0)
                        for a, (zz, xx) in zip(acc, spots)
                    )
                found = lax.fori_loop(0, COLS // SB, weigh, tuple(jnp.zeros((8, SW), jnp.float32) for _ in spots))
                found = [jnp.sum(v, axis=0, keepdims=True) for v in found]
                for zz in range(zg, zg + GZ):
                    s = jnp.concatenate(found[(zz - zg) * NX:(zz - zg + 1) * NX], axis=0)
                    bad = bad + low(s)
                    f_buf[it, row, zz] = m_rows[zz] + shift + jnp.log2(s)
                for zz in range(zg, zg + GZ):
                    send_f(it, zz)
        elif it:
            def again(r, carry):
                def tops_of(i, acc):
                    rows = pl.ds(pl.multiple_of(i * EB, EB), EB)
                    v = zs[r, rows, :] + vrep[rows, :]
                    return jnp.maximum(acc, jnp.max(v.reshape(EB // 8, 8, SW), axis=0))
                top = lax.fori_loop(0, COLS // EB, tops_of, jnp.full((8, SW), -jnp.inf, jnp.float32))
                top = jnp.max(top, axis=0, keepdims=True)

                def sums_of(i, acc):
                    rows = pl.ds(pl.multiple_of(i * EB, EB), EB)
                    v = jnp.exp2((zs[r, rows, :] + vrep[rows, :]) - top)
                    return acc + jnp.sum(v.reshape(EB // 8, 8, SW), axis=0)
                s = lax.fori_loop(0, COLS // EB, sums_of, jnp.zeros((8, SW), jnp.float32))
                f_buf[it, row, r // NX, pl.ds(lax.rem(r, NX), 1), :] = top + jnp.log2(
                    jnp.sum(s, axis=0, keepdims=True))
                return carry
            lax.fori_loop(0, NR, again, 0)
            for zz in range(NZ):
                send_f(it, zz)
        wait_bytes(f_buf.at[it], NR - 1, f_sems.at[it, 1])
        parts = [f_buf[it, r] for r in range(NR)]
        top = functools.reduce(jnp.maximum, parts)
        whole = top + jnp.log2(functools.reduce(jnp.add, [jnp.exp2(v - top) for v in parts]))
        term = a_rows[...] - whole
        level = jnp.zeros((1, 1), jnp.float32)
        if fast:
            term = term + m_rows[...]
            level = all_of(jnp.max(term, axis=0), jnp.max)
            u_rows[...] = jnp.exp2(term - level[None])
        else:
            u_rows[...] = term
        TPH = max(NT // 2, 1)
        for half in range(NT // TPH):
            def tile(i, carry):
                rows = pl.ds(pl.multiple_of((half * TPH + i) * 128, 128), 128)

                def scaled(r):
                    return zs[r, rows, :] * u_rows[r // NX, r % NX:r % NX + 1, :]
                acc = scaled(0)
                for r in range(1, NR):
                    acc = acc + scaled(r)
                wacc[rows, :] = acc
                return carry

            def tile_wide(i, carry):
                rows = pl.ds(pl.multiple_of((half * TPH + i) * 128, 128), 128)

                def moved(r):
                    return zs[r, rows, :] + u_rows[r // NX, r % NX:r % NX + 1, :]
                top = functools.reduce(jnp.maximum, [moved(r) for r in range(NR)])
                top = jnp.max(top, axis=1, keepdims=True)
                acc = functools.reduce(jnp.add, [jnp.exp2(moved(r) - top) for r in range(NR)])
                wacc[rows, :] = jnp.broadcast_to(top + jnp.log2(jnp.sum(acc, axis=1, keepdims=True)), (128, 128))
                return carry
            lax.fori_loop(0, TPH, tile if fast else tile_wide, 0)
            found = []
            for i in range(half * TPH, (half + 1) * TPH):
                turned = wacc[i * 128:(i + 1) * 128, :].T
                found.append(jnp.sum(turned, axis=0, keepdims=True) if fast else turned[0:1, :])
            found = jnp.concatenate(found, axis=0)
            lines = slice(half * TPH, (half + 1) * TPH)
            if fast:
                bad = bad + low(found)
                found = jnp.log2(found) + level
            c_buf[it, col, lines, :] = found - bias[lines, :]
            to_all(col_peer, NK, c_buf.at[it, col, pl.ds(half * TPH, TPH)], c_sems.at[it])
        if last:
            g_tmp[...] = whole
            fo_buf[col] = g_tmp[z, pl.ds(x, 1), :] * (-NATS)
            to_all(col_peer, NK, fo_buf.at[col], fo_sems)
        wait_bytes(c_buf.at[it], NK - 1, c_sems.at[it, 1])
        parts = [c_buf[it, c] for c in range(NK)]
        top = functools.reduce(jnp.maximum, parts)
        mapped = (top + jnp.log2(functools.reduce(jnp.add, [jnp.exp2(v - top) for v in parts]))) * (-NATS)
        images = (images + [mapped])[-HIST:]
        base = (base + [g_now])[-HIST:]
        resid = [p - q for p, q in zip(images, base)]
        prods = [jnp.sum(resid[a] * resid[b], axis=0, keepdims=True) for a, b in pairs]
        prods.append(jnp.where(line == 0, bad, 0.0))
        sums = jnp.sum(jnp.concatenate(prods, axis=0), axis=1, keepdims=True)
        r_buf[it, row] = jnp.sum(jnp.where(eye, sums, 0.0), axis=0, keepdims=True)
        to_all(row_peer, NR, r_buf.at[it, row], r_sems.at[it])
        wait_bytes(r_buf.at[it], NR - 1, r_sems.at[it, 1])
        flat = functools.reduce(jnp.add, [r_buf[it, r] for r in range(NR)])

        def entry(k):
            return jnp.sum(jnp.where(line == k, flat, 0.0), axis=1, keepdims=True)
        mix = solve({ab: entry(k) for k, ab in enumerate(pairs)})
        g_next = functools.reduce(jnp.add, [v * m for v, m in zip(images, mix)])
        if last:
            hist[0] = g_next
            for q in range(TW // 128):
                gout_ref[q:q + 1, :] = hist[0, pl.ds(col * (TW // 128) + q, 1), :]
            flag_ref[...] = jnp.broadcast_to(entry(len(pairs)), (1, 128))
        else:
            delta = (g_next - g_now) * BITS
            if fast:
                shift = all_of(delta, jnp.max)
                delta = jnp.exp2(delta - shift)
            for t in range(NT):
                vrep[t * 128:(t + 1) * 128, :] = jnp.broadcast_to(delta[t:t + 1, :], (128, 128)).T
            g_now = g_next

    wait_bytes(fo_buf, NK - 1, fo_sems.at[1])
    for c in range(NK):
        f_ref[c:c + 1, :] = fo_buf[c]
    wait_bytes(src_all, NR - 1, src_send)
    wait_bytes(tgt_all, NK - 1, tgt_send)
    wait_bytes(fo_buf, NK - 1, fo_sems.at[0])
    for it in range(ITERS):
        wait_bytes(f_buf.at[it], NR - 1, f_sems.at[it, 0])
        wait_bytes(c_buf.at[it], NK - 1, c_sems.at[it, 0])
        wait_bytes(r_buf.at[it], NR - 1, r_sems.at[it, 0])


def shards(dims, src, tgt, log_a, log_b, g, hist_g, hist_maps):
    NZ, NX, NY, NC = dims
    NR, NK = NZ * NX, NY * NC
    D, SW = src.shape
    TW = tgt.shape[1]
    COLS = NK * TW
    NT = COLS // 128
    f32 = jnp.float32
    vmem = pl.BlockSpec(memory_space=pltpu.VMEM)
    dma = pltpu.SemaphoreType.DMA

    def call(fast):
        return pl.pallas_call(
            functools.partial(kernel, fast, dims),
            out_shape=(
                jax.ShapeDtypeStruct((NK, SW), f32),
                jax.ShapeDtypeStruct((TW // 128, 128), f32),
                jax.ShapeDtypeStruct((1, 128), f32),
            ),
            in_specs=[pl.BlockSpec(memory_space=pltpu.HBM)] * 7,
            out_specs=(vmem, vmem, vmem),
            scratch_shapes=[
                pltpu.VMEM((NR, D + 8, SW), f32),
                pltpu.VMEM((NK, D + 16, TW), f32),
                pltpu.VMEM((NK, SW), f32),
                pltpu.VMEM((1, TW), f32),
                pltpu.VMEM((1, TW), f32),
                pltpu.VMEM((HIST - 1, TW), f32),
                pltpu.VMEM((HIST - 1, TW), f32),
                pltpu.VMEM((COLS, 4 * D), jnp.bfloat16),
                pltpu.VMEM((NR, COLS, SW), f32),
                pltpu.VMEM((COLS, 128), f32),
                pltpu.VMEM((COLS, 128), f32),
                pltpu.VMEM((2 * HIST, NT, 128), f32),
                pltpu.VMEM((NZ, NX, SW), f32),
                pltpu.VMEM((NZ, NX, SW), f32),
                pltpu.VMEM((NZ, NX, SW), f32),
                pltpu.VMEM((NZ, NX, SW), f32),
                pltpu.VMEM((ITERS, NR, NZ, NX, SW), f32),
                pltpu.VMEM((NK, 1, SW), f32),
                pltpu.VMEM((ITERS, NK, NT, 128), f32),
                pltpu.VMEM((ITERS, NR, 1, 128), f32),
                dma((7,)), dma, dma((2, NR)), dma, dma((NK,)),
                dma((ITERS, 2)), dma((2,)), dma((ITERS, 2)), dma((ITERS, 2)),
            ],
            compiler_params=pltpu.CompilerParams(
                collective_id=0 if fast else 1, has_side_effects=True, vmem_limit_bytes=48 * 1024 * 1024
            ),
            name="sinkhorn" if fast else "sinkhorn_wide",
        )(src, tgt, log_a.reshape(NK, SW), log_b.reshape(NR, 1, TW), g.reshape(1, TW), hist_g, hist_maps)

    f, gout, flag = call(True)
    f, gout = lax.cond(flag[0, 0] > 0.5, lambda: call(False)[:2], lambda: (f, gout))
    return f.reshape(-1), gout.reshape(-1)


def solution(mesh, dims=(4, 4, 4, 2)):
    grid = Mesh(mesh.devices.reshape(dims), AXES)
    in_specs = (
        P(None, AXES),
        P(None, ("y", "core", "z", "x")),
        P(("z", "x")),
        P(("y", "core")),
        P(("y", "core", "z", "x")),
        P(None, ("y", "core", "z", "x")),
        P(None, ("y", "core", "z", "x")),
    )
    out_specs = (P(("z", "x")), P(("y", "core", "z", "x")))
    return jax.shard_map(
        functools.partial(shards, dims), mesh=grid, in_specs=in_specs, out_specs=out_specs, check_vma=False
    )
```

time: 93.6 us -> 134 us (1.43)
  Pallas kernels: 87.1 us -> 130 us
  local copies, waits for them, and re-layouts: 5.52 us -> 2.47 us
    pallas_call x1 -> x2, Pallas kernels: 87.1 us -> 130 us  [call(): pl.pallas_call(functools.partial(kernel, fast, dims), out_shape=(jax.Shap...]
    unnamed x16, local copies, waits for them, and re-layouts: 5.52 us -> 2.47 us
where the time goes in v4:
time: 134 us
  Pallas kernels  130 us (97%)
  local copies, waits for them, and re-layouts  2.47 us (2%)
    pallas_call x2, Pallas kernels, call(): pl.pallas_call(functools.partial(kernel, fast, dims), out_shape=(jax.Shap...  130 us

profile of v4, /device:TPU:1, one launch (start us, length us, event | category | flops | bytes accessed | tf_op | source)
XLA Modules:
  0.0 133.7 jit_solution(7511375116311749156)
XLA Ops:
  0.6 0.0 copy-start.3
  0.6 0.0 copy-start.6
  0.7 0.7 copy-done.3
  1.3 0.0 copy-done.6
  1.3 0.0 copy-start
  1.3 0.0 copy-start.1
  1.3 0.0 copy-start.2
  1.3 60.4 %sinkhorn.1 = (f32[8,128]{1,0:T(8,128)S(1)}, f32[2,128]{1,0:T(2,128)S(1)}, f32[1,128]{1,0:T(1,128)S(1)}) custom-call(f32[64,128]{1,0:T(8,128)} %src_hbm.1, f32[64,256]{1,0:T(8,128)} %tgt_hbm.1, f32[8,128]{1,0:T(8,128)S(1)} %bitcast.15, f32[16,1,256]{2,1,0:T(1,128)} %bitcast.13, f32[1,256]{1,0:T(1,128)S(1)} %bitcast.17, f32[4,256]{1,0:T(4,128)} %hg_hbm.1, ...), custom_call_target="tpu_custom_call" | custom-call | tf_op jit(solution)/shard_map/sinkhorn/pallas_call | solution.py:480
  61.7 0.0 copy-start.5
  61.7 0.0 copy-start.4
  61.8 0.0 copy-done
  61.8 0.0 copy-done.1
  61.8 0.0 copy-done.2
  61.8 0.6 copy-done.5
  62.4 0.0 copy-done.4
  62.4 70.1 %conditional.1 = (f32[1024]{0:T(1024)S(1)}, f32[256]{0:T(256)S(1)}) conditional(s32[]{:T(128)} %bitcast.10, (f32[8,128]{1,0:T(8,128)S(1)}, f32[2,128]{1,0:T(2,128)S(1)}) %tuple.30, (f32[1024]{0:T(1024)S(1)}, f32[4096]{0:T(1024)S(1)}, f32[256]{0:T(256)S(1)}, f32[64,128]{1,0:T(8,128)S(1)}, f32[64,256]{1,0:T(8,128)S(1)}, ...), branch_computations={%region_0.0_spmd, %region_1.0_spmd} | conditional | bytes 16 | solution.py:520
  62.4 70.1 %sinkhorn_wide.1 = (f32[8,128]{1,0:T(8,128)S(1)}, f32[2,128]{1,0:T(2,128)S(1)}, f32[1,128]{1,0:T(1,128)}) custom-call(f32[64,128]{1,0:T(8,128)S(1)} %get-tuple-element.24.src_hbm, f32[64,256]{1,0:T(8,128)S(1)} %get-tuple-element.25.tgt_hbm, f32[8,128]{1,0:T(8,128)S(1)} %bitcast.16, f32[16,1,256]{2,1,0:T(1,128)S(1)} %bitcast.14, f32[1,256]{1,0:T(1,128)S(1)} %bitcast.18, ...), custom_call_target="tpu_custom_call" | custom-call | tf_op jit(solution)/shard_map/cond/branch_1_fun/sinkhorn_wide/pallas_call | solution.py:480
  132.5 0.6 copy.17
  133.1 0.6 copy.18
Async XLA Ops:
  0.6 0.7 copy-start.3
  0.6 0.7 copy-start.6
  1.3 60.5 %copy-start = (f32[64,256]{1,0:T(8,128)S(1)}, f32[64,256]{1,0:T(8,128)}, u32[]{:S(2)}) copy-start(f32[64,256]{1,0:T(8,128)} %tgt_hbm.1) | copy-start | bytes 196612
  1.3 60.5 %copy-start.1 = (f32[64,128]{1,0:T(8,128)S(1)}, f32[64,128]{1,0:T(8,128)}, u32[]{:S(2)}) copy-start(f32[64,128]{1,0:T(8,128)} %src_hbm.1) | copy-start | bytes 98308
  1.3 60.5 %copy-start.2 = (f32[4096]{0:T(1024)S(1)}, f32[4096]{0:T(1024)}, u32[]{:S(2)}) copy-start(f32[4096]{0:T(1024)} %param.12) | copy-start | bytes 49156
  61.7 0.7 copy-start.5
  61.7 0.7 copy-start.4

commit v5 on v4

--- a/solution.py
+++ b/solution.py
@@ -71,7 +71,7 @@
     src_hbm, tgt_hbm, loga_hbm, logb_hbm, g_hbm, hg_hbm, hm_hbm,
     f_ref, gout_ref, flag_ref,
     src_all, tgt_all, loga_in, logb_in, g_in, hg_in, hm_in,
-    left, zs, wacc, vrep, hist, m_rows, a_rows, u_rows, g_tmp,
+    left, staged, tops_buf, zs, wacc, vrep, hist, m_rows, a_rows, u_rows, g_tmp,
     f_buf, fo_buf, c_buf, r_buf,
     in_sems, src_send, src_recv, tgt_send, tgt_recv, f_sems, fo_sems, c_sems, r_sems,
 ):
@@ -103,10 +103,8 @@
         ).start()
 
     def to_all(peer, count, part, sems):
-        def one(k, carry):
+        for k in range(1, count):
             remote(part, sems.at[0], sems.at[1], peer(k))
-            return carry
-        lax.fori_loop(1, count, one, 0)
 
     def wait_for(part, sem):
         pltpu.make_async_copy(part, part, sem).wait()
@@ -140,67 +138,81 @@
     pl.semaphore_wait(barrier, len(around))
 
     HALF, QUART, EXTRA = D // 2, D // 4, 8
-    PIECES = {
-        (0, None): (0, HALF), (0, 0): (0, QUART), (0, 1): (QUART, QUART),
-        (1, None): (HALF, HALF + EXTRA), (1, 0): (HALF, QUART + EXTRA), (1, 1): (HALF + QUART + EXTRA, QUART),
-    }
+    PIECES = (((0, QUART), (QUART, QUART)), ((HALF, QUART + EXTRA), (HALF + QUART + EXTRA, QUART)))
     ORDER = (("x", "z"), ("z", "x"))
+    seen = set()
 
     def slot_of(dz, dx):
         return lax.rem(z + dz + NZ, NZ) * NX + lax.rem(x + dx + NX, NX)
 
-    def piece(r, h, sub=None):
-        start, count = PIECES[h, sub]
+    def piece(r, h, sub):
+        start, count = PIECES[h][sub]
         return src_all.at[r, pl.ds(start, count)]
 
     def pass_on(r, h, sub, axis, d):
-        remote(piece(r, h, sub), src_send, src_recv.at[h, r], near(axis, d))
-
-    def arrived(h, da, db):
+        remote(piece(r, h, sub), src_send, src_recv.at[h, sub, r], near(axis, d))
+
+    def part_for(d):
+        return 0 if d < 0 else 1
+
+    def start_sources():
+        for phase in (0, 1):
+            for first in (True, False):
+                for h in (0, 1):
+                    axis = ORDER[h][phase]
+                    if SIZE[axis] > 1:
+                        for d in (1, -1):
+                            pass_on(row, h, part_for(-d) if first else part_for(d), axis, d)
+
+    def arrived(h, da, db, sub):
         a, b = ORDER[h]
-        if (da and SIZE[a] == 1) or (db and SIZE[b] == 1):
+        if (h, da, db, sub) in seen or (da == 0 and db == 0):
             return
+        seen.add((h, da, db, sub))
         r = slot_of(**{"d" + a: da, "d" + b: db})
-        if da or db:
-            wait_for(piece(r, h), src_recv.at[h, r])
+        wait_for(piece(r, h, sub), src_recv.at[h, sub, r])
         if db == 0:
-            if da == 0 and SIZE[a] > 1:
-                for d in (1, -1):
-                    pass_on(r, h, None, a, d)
-            elif da in (1, -1):
-                pass_on(r, h, 0 if da < 0 else 1, a, -da)
-            if SIZE[b] > 1:
-                for d in (1, -1):
-                    pass_on(r, h, None, b, d)
-        elif db in (1, -1):
-            pass_on(r, h, 0 if db < 0 else 1, b, -db)
-
-    TROWS = D + 16
-
-    def target(c, sub=None):
-        if sub is None:
-            return tgt_all.at[c]
-        return tgt_all.at[c, pl.ds(sub * (TROWS // 2), TROWS // 2)]
+            if da in (1, -1) and sub == part_for(da):
+                pass_on(r, h, sub, a, -da)
+            for d in (1, -1):
+                pass_on(r, h, sub, b, d)
+        elif db in (1, -1) and sub == part_for(db):
+            pass_on(r, h, sub, b, -db)
+
+    def complete(*blocks):
+        for dz, dx in blocks:
+            for h in (0, 1):
+                da, db = (dx, dz) if h == 0 else (dz, dx)
+                for sub in (0, 1):
+                    arrived(h, da, db, sub)
+
+    THALF = (D + 16) // 2
+
+    def target(c, sub):
+        return tgt_all.at[c, pl.ds(sub * THALF, THALF)]
 
     def tgt_slot(dy, other=0):
         return lax.rem(y + dy + NY, NY) * NC + lax.rem(core + other, NC)
 
     def tgt_pass(c, sub, axis, d):
-        remote(target(c, sub), tgt_send, tgt_recv.at[c], near(axis, d))
-
-    def tgt_arrived(dy):
-        if dy and NY == 1:
-            return
+        remote(target(c, sub), tgt_send, tgt_recv.at[sub, c], near(axis, d))
+
+    def start_targets():
+        if NY > 1:
+            for first in (True, False):
+                for d in (1, -1):
+                    tgt_pass(col, part_for(-d) if first else part_for(d), "y", d)
+        if NC > 1:
+            for sub in (0, 1):
+                tgt_pass(col, sub, "core", 1)
+
+    def tgt_arrived(dy, sub):
         c = tgt_slot(dy)
-        if dy:
-            wait_for(target(c), tgt_recv.at[c])
-        if dy == 0 and NY > 1:
-            for d in (1, -1):
-                tgt_pass(c, None, "y", d)
-        elif dy in (1, -1):
-            tgt_pass(c, 0 if dy < 0 else 1, "y", -dy)
+        wait_for(target(c, sub), tgt_recv.at[sub, c])
+        if dy in (1, -1) and sub == part_for(dy):
+            tgt_pass(c, sub, "y", -dy)
         if NC > 1:
-            tgt_pass(c, None, "core", 1)
+            tgt_pass(c, sub, "core", 1)
 
     def take_targets(c):
         v = tgt_all[c, 0:D, :]
@@ -220,38 +232,51 @@
         tail = placed(D, [one] * 6 + list(split3(norm)), SW)
         return jnp.concatenate([hi, hi, lo, tail], axis=0).astype(jnp.bfloat16)
 
+    QB = min(512, COLS)
     EB = min(256, COLS)
 
-    def block(offsets):
-        spots = [(lax.rem(z + dz + NZ, NZ), lax.rem(x + dx + NX, NX)) for dz, dx in offsets]
-        slots = [zb * NX + xb for zb, xb in spots]
-        t = jnp.dot(
-            left[...], jnp.concatenate([sources(r) for r in slots], axis=1), preferred_element_type=jnp.float32
-        )
-        tops = []
-        for n, r in enumerate(slots):
-            part = t[:, n * SW:(n + 1) * SW]
-            zs[r] = part
-            tops.append(jnp.max(jnp.max(part.reshape(COLS // 8, 8, SW), axis=0), axis=0, keepdims=True))
-
-        def expo(i, acc):
-            rows = pl.ds(pl.multiple_of(i * EB, EB), EB)
-            out = []
-            for n, r in enumerate(slots):
-                e = jnp.exp2(zs[r, rows, :] - tops[n])
+    def spots_of(offsets):
+        return [(lax.rem(z + dz + 8 * NZ, NZ), lax.rem(x + dx + 8 * NX, NX)) for dz, dx in offsets]
+
+    def folded(v, op):
+        return op(v.reshape(v.shape[0] // 8, 8, v.shape[1]), axis=0)
+
+    def step(done, new):
+        if new:
+            right = jnp.concatenate([sources(zb * NX + xb) for zb, xb in new], axis=1)
+        tops, sums = [None] * len(new), [None] * len(done)
+        before = [tops_buf[n] for n in range(len(done))]
+        for q in range(COLS // QB):
+            rows = slice(q * QB, (q + 1) * QB)
+            for n, (zb, xb) in enumerate(done):
+                e = jnp.exp2(staged[rows, n * SW:(n + 1) * SW] - before[n])
                 if fast:
-                    zs[r, rows, :] = e
-                out.append(acc[n] + jnp.sum(e.reshape(EB // 8, 8, SW), axis=0))
-            return tuple(out)
-        found = lax.fori_loop(0, COLS // EB, expo, tuple(jnp.zeros((8, SW), jnp.float32) for _ in slots))
-        for n, (zb, xb) in enumerate(spots):
-            f_buf[0, row, zb, pl.ds(xb, 1), :] = tops[n] + jnp.log2(jnp.sum(found[n], axis=0, keepdims=True))
-            m_rows[zb, pl.ds(xb, 1), :] = tops[n]
-            a_rows[zb, pl.ds(xb, 1), :] = src_all[slots[n], D:D + 1, :] * LOG2E
-
-    def blocks(count, offsets):
+                    zs[zb * NX + xb, rows, :] = e
+                else:
+                    zs[zb * NX + xb, rows, :] = staged[rows, n * SW:(n + 1) * SW]
+                e = folded(e, jnp.sum)
+                sums[n] = e if q == 0 else sums[n] + e
+            if new:
+                t = jnp.dot(left[rows, :], right, preferred_element_type=jnp.float32)
+                staged[rows, 0:len(new) * SW] = t
+                for n in range(len(new)):
+                    top = folded(t[:, n * SW:(n + 1) * SW], jnp.max)
+                    tops[n] = top if q == 0 else jnp.maximum(tops[n], top)
+        for n, (zb, xb) in enumerate(done):
+            f_buf[0, row, zb, pl.ds(xb, 1), :] = before[n] + jnp.log2(jnp.sum(sums[n], axis=0, keepdims=True))
+            m_rows[zb, pl.ds(xb, 1), :] = before[n]
+            a_rows[zb, pl.ds(xb, 1), :] = src_all[zb * NX + xb, D:D + 1, :] * LOG2E
+        for n in range(len(new)):
+            tops_buf[n] = jnp.max(tops[n], axis=0, keepdims=True)
+
+    def steps(count, first, offsets, after=None):
         def one(k, carry):
-            block(offsets(k))
+            p = jnp.minimum(k, 1)
+            before = offsets(jnp.maximum(k - 1, 0))
+            before = [tuple(p * v + (1 - p) * w for v, w in zip(*pair)) for pair in zip(before, first)]
+            step(spots_of(before), spots_of(offsets(k)))
+            if after is not None:
+                after(k)
             return carry
         lax.fori_loop(0, count, one, 0)
 
@@ -259,51 +284,79 @@
         to_all(row_peer, NR, f_buf.at[it, row, zb], f_sems.at[it])
 
     both = NZ > 1 and NX > 1
-    tgt_arrived(0)
-    for h in (0, 1):
-        arrived(h, 0, 0)
+    start_sources()
+    start_targets()
     take_targets(col)
-    for dy in (1, -1):
-        tgt_arrived(dy)
-    for h in (0, 1):
-        for da in (1, -1):
-            arrived(h, da, 0)
-    for h in (0, 1):
-        for db in (1, -1):
-            arrived(h, 0, db)
-    tgt_arrived(2)
+    if both:
+        for h in (0, 1):
+            for d in (1, -1):
+                arrived(h, d, 0, part_for(d))
+        for h in (0, 1):
+            for d in (1, -1):
+                arrived(h, d, 0, part_for(-d))
     if NY > 1:
+        for d in (1, -1):
+            tgt_arrived(d, part_for(d))
+        for d in (1, -1):
+            tgt_arrived(d, part_for(-d))
+    if both:
+        for h in (0, 1):
+            for d in (1, -1):
+                arrived(h, 0, d, part_for(d))
+    if both:
+        for h in (0, 1):
+            for sub in (0, 1):
+                arrived(h, 2, 0, sub)
+            for da in (1, -1):
+                for db in (1, -1):
+                    arrived(h, da, db, part_for(db))
+    if NY > 1:
+        for sub in (0, 1):
+            tgt_arrived(2, sub)
         for dy in (1, -1, 2):
             take_targets(tgt_slot(dy))
-    for h in (0, 1):
-        arrived(h, 2, 0)
-        for da in (1, -1):
-            for db in (1, -1):
-                arrived(h, da, db)
     if NC > 1:
         for dy in ((0, 1, -1, 2) if NY > 1 else (0,)):
             c = tgt_slot(dy, 1)
-            wait_for(target(c), tgt_recv.at[c])
+            for sub in (0, 1):
+                wait_for(target(c, sub), tgt_recv.at[sub, c])
             take_targets(c)
     if both:
-        blocks(2, lambda k: ((k, 1 - k), (-k, k - 1)))
-    for h in (0, 1):
-        for db in (1, -1):
-            arrived(h, 2, db)
-        arrived(h, 0, 2)
-    if both:
-        blocks(2, lambda k: ((1, 1 - 2 * k), (-1, 1 - 2 * k)))
-    block(((0, 0), (0, 2)) if both else ((0, 0),))
-    for h in (0, 1):
-        for da in (1, -1, 2):
-            arrived(h, da, 2)
-    send_f(0, z)
-    if both:
-        blocks(1, lambda k: ((1, 2), (-1, 2)))
-        for d in (1, 3):
-            send_f(0, lax.rem(z + d, NZ))
-        blocks(2, lambda k: ((2, 1 - k), (2, 3 * k - 1)))
-        send_f(0, lax.rem(z + 2, NZ))
+        complete((0, 1), (0, -1), (1, 0), (-1, 0))
+    PAIR_A, PAIR_B = ((0, 1), (0, -1)), ((1, 0), (-1, 0))
+    step([], spots_of(PAIR_A if both else ((0, 0),)))
+    if both:
+        step(spots_of(PAIR_A), spots_of(PAIR_B))
+    if both:
+        for h in (0, 1):
+            for db in (1, -1):
+                arrived(h, 2, db, part_for(db))
+    if both:
+        complete((1, 1), (1, -1), (-1, 1), (-1, -1), (0, 2))
+    if both:
+        def mid(k):
+            a = 1 - k // 2
+            return (a, (1 - 2 * k) * a), (-a, (1 - 2 * k) * a + 2 - 2 * a)
+        steps(3, PAIR_B, mid)
+    if both:
+        complete((1, 2), (-1, 2), (2, 1), (2, -1), (2, 0), (2, 2))
+    if both:
+        def end(k):
+            a = (2 - k) // 2
+            return (2 - a, 2 - k), (2 - 3 * a, 2 - 3 * lax.rem(k, 2))
+
+        def ready(k):
+            @pl.when(k == 0)
+            def _():
+                send_f(0, z)
+
+            @pl.when(k == 1)
+            def _():
+                for d in (1, 3):
+                    send_f(0, lax.rem(z + d, NZ))
+        steps(3, ((0, 0), (0, 2)), end, ready)
+    step(spots_of(((2, 0), (2, 2)) if both else ((0, 0),)), [])
+    send_f(0, lax.rem(z + NZ // 2, NZ))
     for c in range(NK):
         for k in range(2 * KEPT + 2):
             for q in range(TW // 128):
@@ -495,6 +548,8 @@
                 pltpu.VMEM((HIST - 1, TW), f32),
                 pltpu.VMEM((HIST - 1, TW), f32),
                 pltpu.VMEM((COLS, 4 * D), jnp.bfloat16),
+                pltpu.VMEM((COLS, 2 * SW), f32),
+                pltpu.VMEM((2, 1, SW), f32),
                 pltpu.VMEM((NR, COLS, SW), f32),
                 pltpu.VMEM((COLS, 128), f32),
                 pltpu.VMEM((COLS, 128), f32),
@@ -507,7 +562,7 @@
                 pltpu.VMEM((NK, 1, SW), f32),
                 pltpu.VMEM((ITERS, NK, NT, 128), f32),
                 pltpu.VMEM((ITERS, NR, 1, 128), f32),
-                dma((7,)), dma, dma((2, NR)), dma, dma((NK,)),
+                dma((7,)), dma, dma((2, 2, NR)), dma, dma((2, NK)),
                 dma((ITERS, 2)), dma((2,)), dma((ITERS, 2)), dma((ITERS, 2)),
             ],
             compiler_params=pltpu.CompilerParams(

time: 134 us -> 126 us (0.940)
  Pallas kernels: 130 us -> 122 us
    pallas_call x2, Pallas kernels: 130 us -> 122 us  [call(): pl.pallas_call(functools.partial(kernel, fast, dims), out_shape=(jax.Shap...]
where the time goes in v5:
time: 126 us
  Pallas kernels  122 us (97%)
  local copies, waits for them, and re-layouts  2.47 us (2%)
    pallas_call x2, Pallas kernels, call(): pl.pallas_call(functools.partial(kernel, fast, dims), out_shape=(jax.Shap...  122 us

profile of v5, /device:TPU:1, one launch (start us, length us, event | category | flops | bytes accessed | tf_op | source)
XLA Modules:
  0.0 125.7 jit_solution(15294179256076543896)
XLA Ops:
  0.6 0.0 copy-start.3
  0.6 0.0 copy-start.6
  0.7 0.7 copy-done.3
  1.3 0.0 copy-done.6
  1.3 0.0 copy-start
  1.3 0.0 copy-start.1
  1.3 0.0 copy-start.2
  1.3 56.5 %sinkhorn.1 = (f32[8,128]{1,0:T(8,128)S(1)}, f32[2,128]{1,0:T(2,128)S(1)}, f32[1,128]{1,0:T(1,128)S(1)}) custom-call(f32[64,128]{1,0:T(8,128)} %src_hbm.1, f32[64,256]{1,0:T(8,128)} %tgt_hbm.1, f32[8,128]{1,0:T(8,128)S(1)} %bitcast.15, f32[16,1,256]{2,1,0:T(1,128)} %bitcast.13, f32[1,256]{1,0:T(1,128)S(1)} %bitcast.17, f32[4,256]{1,0:T(4,128)} %hg_hbm.1, ...), custom_call_target="tpu_custom_call" | custom-call | tf_op jit(solution)/shard_map/sinkhorn/pallas_call | solution.py:533
  57.8 0.0 copy-start.5
  57.8 0.0 copy-start.4
  57.9 0.0 copy-done
  57.9 0.0 copy-done.1
  57.9 0.0 copy-done.2
  57.9 0.6 copy-done.5
  58.5 0.0 copy-done.4
  58.5 66.0 %conditional.1 = (f32[1024]{0:T(1024)S(1)}, f32[256]{0:T(256)S(1)}) conditional(s32[]{:T(128)} %bitcast.10, (f32[8,128]{1,0:T(8,128)S(1)}, f32[2,128]{1,0:T(2,128)S(1)}) %tuple.30, (f32[1024]{0:T(1024)S(1)}, f32[4096]{0:T(1024)S(1)}, f32[256]{0:T(256)S(1)}, f32[64,128]{1,0:T(8,128)S(1)}, f32[64,256]{1,0:T(8,128)S(1)}, ...), branch_computations={%region_0.0_spmd, %region_1.0_spmd} | conditional | bytes 16 | solution.py:575
  58.5 66.0 %sinkhorn_wide.1 = (f32[8,128]{1,0:T(8,128)S(1)}, f32[2,128]{1,0:T(2,128)S(1)}, f32[1,128]{1,0:T(1,128)}) custom-call(f32[64,128]{1,0:T(8,128)S(1)} %get-tuple-element.24.src_hbm, f32[64,256]{1,0:T(8,128)S(1)} %get-tuple-element.25.tgt_hbm, f32[8,128]{1,0:T(8,128)S(1)} %bitcast.16, f32[16,1,256]{2,1,0:T(1,128)S(1)} %bitcast.14, f32[1,256]{1,0:T(1,128)S(1)} %bitcast.18, ...), custom_call_target="tpu_custom_call" | custom-call | tf_op jit(solution)/shard_map/cond/branch_1_fun/sinkhorn_wide/pallas_call | solution.py:533
  124.5 0.6 copy.17
  125.1 0.6 copy.18
Async XLA Ops:
  0.6 0.7 copy-start.3
  0.6 0.7 copy-start.6
  1.3 56.6 %copy-start = (f32[64,256]{1,0:T(8,128)S(1)}, f32[64,256]{1,0:T(8,128)}, u32[]{:S(2)}) copy-start(f32[64,256]{1,0:T(8,128)} %tgt_hbm.1) | copy-start | bytes 196612
  1.3 56.6 %copy-start.1 = (f32[64,128]{1,0:T(8,128)S(1)}, f32[64,128]{1,0:T(8,128)}, u32[]{:S(2)}) copy-start(f32[64,128]{1,0:T(8,128)} %src_hbm.1) | copy-start | bytes 98308
  1.3 56.6 %copy-start.2 = (f32[4096]{0:T(1024)S(1)}, f32[4096]{0:T(1024)}, u32[]{:S(2)}) copy-start(f32[4096]{0:T(1024)} %param.12) | copy-start | bytes 49156
  57.8 0.7 copy-start.5
  57.8 0.7 copy-start.4
